TPU v7x, 512 devices: a whole 4x8x8 slice. The times are simulated.
512 devices in a mesh: depth: 32 (over x, y), rows: 16 (over z, core).
Axes of the slice: x: 4, y: 8, z: 8, core: 2. Of those that a mesh axis runs over, the one named last changes fastest.
Arguments:
- ref_feat: bfloat16 [2, 32, 5120], P(None, 'rows'), may hold values from -6 to 6
- src_feat: bfloat16 [2, 4, 32, 5120], P(None, None, 'rows'), may hold values from -6 to 6
- block_index: int32 [2, 4, 192, 16], P(None, None, 'depth', 'rows'), may hold values from 0 to 14, as said below
- blend: bfloat16 [2, 4, 192, 32, 160], P(None, None, 'depth', 'rows'), may hold values from 0 to 1
- conv_first: bfloat16 [3, 3, 3, 32, 40], replicated, may hold values from -0.1875 to 0.1875
- bias_first: float32 [32], replicated, may hold values from -3 to 3
- conv_second: bfloat16 [3, 3, 3, 32, 32], replicated, may hold values from -0.21875 to 0.21875
- bias_second: float32 [32], replicated, may hold values from -3 to 3
Outputs:
- regularized: bfloat16 [2, 192, 32, 5120], P(None, 'depth', 'rows')
Inputs may be any that keep to these rules, and one draw needn't show every extreme that they name: block_index[b, v, d, q] is q - 1 or q, held within 0 to 14, so rows of block q blend source row blocks block_index and block_index + 1.
All inputs are finite; a program needn't handle non-finite values.
Results may differ from a plain program's by a relative error of at most 0.0046.
Values may be sent and summed in bfloat16 or wider, within the bound.
No kernel may reach another device: no remote copies, remote signals or barrier semaphores. Data moves between devices by JAX's collectives and lax.ppermute only.
A program may use at most 64 MiB of HBM per device.

v0:
```python
import jax
import jax.numpy as jnp
from jax import lax
from jax.sharding import PartitionSpec as P


def extended(block, sides, width):
    for axis, dim in sides:
        count = lax.axis_size(axis)
        forward = [(i, i + 1) for i in range(count - 1)]
        backward = [(target, source) for source, target in forward]
        low = lax.ppermute(
            lax.slice_in_dim(block, block.shape[dim] - width, None, axis=dim), axis, forward
        )
        high = lax.ppermute(lax.slice_in_dim(block, 0, width, axis=dim), axis, backward)
        block = jnp.concatenate([low, block, high], axis=dim)
    return block


def cost_plane(ref_rows, top_rows, bottom_rows, weight, feat_count, columns, groups):
    scenes = top_rows.shape[0]
    source_views = top_rows.shape[1]
    row_count = top_rows.shape[2]
    reference_cube = ref_rows.astype(jnp.float32).reshape(scenes, 1, row_count, feat_count, columns)
    blend_weight = weight.astype(jnp.float32)[:, :, :, None, :]
    upper_part = top_rows.astype(jnp.float32).reshape(
        scenes, source_views, row_count, feat_count, columns
    )
    lower_part = bottom_rows.astype(jnp.float32).reshape(
        scenes, source_views, row_count, feat_count, columns
    )
    warped = blend_weight * upper_part + (1.0 - blend_weight) * lower_part
    average = (reference_cube[:, 0] + jnp.sum(warped, axis=1)) / (source_views + 1.0)
    spread = (
        (reference_cube[:, 0] - average) ** 2 + jnp.sum((warped - average[:, None]) ** 2, axis=1)
    ) / (source_views + 1.0)
    per_group = feat_count // groups
    products = (reference_cube * warped).reshape(
        scenes, source_views, row_count, groups, per_group, columns
    )
    correlation = jnp.sum(products, axis=(1, 4)) / (source_views * per_group * 1.0)
    stacked = jnp.concatenate([correlation, spread], axis=2).astype(jnp.bfloat16)
    return stacked.reshape(scenes, row_count, (groups + feat_count) * columns)


def convolve(volume, kernel, shift_bias, out_planes, out_rows, columns):
    scenes = volume.shape[0]
    channels = kernel.shape[4]
    shaped = volume.reshape(scenes, volume.shape[1], volume.shape[2], channels, columns)
    padded = jnp.pad(shaped, ((0, 0), (0, 0), (0, 0), (0, 0), (1, 1)))
    summed = jnp.zeros((scenes, out_planes, out_rows, kernel.shape[3], columns), jnp.float32)
    for tap_depth in range(3):
        for tap_row in range(3):
            for tap_col in range(3):
                piece = padded[
                    :,
                    tap_depth : tap_depth + out_planes,
                    tap_row : tap_row + out_rows,
                    :,
                    tap_col : tap_col + columns,
                ]
                summed = summed + jnp.einsum(
                    "bprcw,oc->bprow",
                    piece,
                    kernel[tap_depth, tap_row, tap_col],
                    preferred_element_type=jnp.float32,
                )
    return summed + shift_bias[None, None, None, :, None]


def body(ref_feat, src_feat, block_index, blend, conv_first, bias_first, conv_second, bias_second):
    scenes = src_feat.shape[0]
    row_count = src_feat.shape[2]
    packed = src_feat.shape[3]
    planes = blend.shape[2]
    columns = blend.shape[4]
    channels = conv_first.shape[4]
    feat_count = packed // columns
    groups = channels - feat_count
    nearby = extended(src_feat, (("rows", 2),), row_count)
    lower_rim = nearby[:, :, :row_count]
    upper_rim = nearby[:, :, 2 * row_count :]
    offset = block_index[:, :, :, 0] - lax.axis_index("rows")

    def plane_cost(inputs):
        plane_offset, weight = inputs
        below = (plane_offset < 0)[:, :, None, None]
        top_rows = jnp.where(below, lower_rim, src_feat)
        bottom_rows = jnp.where(below, src_feat, upper_rim)
        return cost_plane(ref_feat, top_rows, bottom_rows, weight, feat_count, columns, groups)

    cost_planes = lax.map(plane_cost, (jnp.moveaxis(offset, 2, 0), jnp.moveaxis(blend, 2, 0)))
    volume = jnp.moveaxis(cost_planes, 0, 1)
    margin = extended(volume, (("depth", 1), ("rows", 2)), 1)
    hidden = jnp.maximum(convolve(margin, conv_first, bias_first, planes, row_count, columns), 0.0)
    hidden = hidden.astype(jnp.bfloat16).reshape(scenes, planes, row_count, -1)
    hidden_wide = extended(hidden, (("depth", 1), ("rows", 2)), 1)
    result = convolve(hidden_wide, conv_second, bias_second, planes, row_count, columns)
    return result.astype(jnp.bfloat16).reshape(scenes, planes, row_count, -1)


def solution(mesh):
    in_specs = (
        P(None, "rows", None),
        P(None, None, "rows", None),
        P(None, None, "depth", "rows"),
        P(None, None, "depth", "rows", None),
        P(),
        P(),
        P(),
        P(),
    )
    out_specs = P(None, "depth", "rows", None)
    return jax.shard_map(body, mesh=mesh, in_specs=in_specs, out_specs=out_specs, check_vma=False)
```

profile of v0, /device:TPU:215, one launch (start us, length us, event | category | flops | bytes accessed | tf_op | source)
XLA Modules:
  0.0 116.0 jit_solution(17873165881406751426)
XLA Ops:
  0.0 5.8 %collective-permute-start = (bf16[2,4,2,5120]{3,2,1,0:T(2,128)(2,1)}, bf16[2,4,2,5120]{3,2,1,0:T(2,128)(2,1)S(1)}, u32[]{:S(2)}, u32[]{:S(2)}) collective-permute-start(bf16[2,4,2,5120]{3,2,1,0:T(2,128)(2,1)} %param.11), channel_id=1, source_target_pairs={{0,1},{1,2},{2,3},{3,4},{4,5},{5,6},{6,7},{7,8},{8,9},{9,10},{10,1... | collective-permute-start | bytes 491528 | tf_op jit(solution)/shard_map/ppermute | solution.py:12
  5.8 1.9 %collective-permute-start.1 = (bf16[2,4,2,5120]{3,2,1,0:T(2,128)(2,1)}, bf16[2,4,2,5120]{3,2,1,0:T(2,128)(2,1)S(1)}, u32[]{:S(2)}, u32[]{:S(2)}) collective-permute-start(bf16[2,4,2,5120]{3,2,1,0:T(2,128)(2,1)} %param.11), channel_id=1, source_target_pairs={{1,0},{2,1},{3,2},{4,3},{5,4},{6,5},{7,6},{8,7},{9,8},{10,9},{11,1... | collective-permute-start | bytes 491528 | tf_op jit(solution)/shard_map/ppermute | solution.py:15
  7.7 0.8 copy.67
  8.6 0.7 broadcast_subtract_fusion.1
  9.4 4.5 %collective-permute-done.1 = bf16[2,4,2,5120]{3,2,1,0:T(2,128)(2,1)S(1)} collective-permute-done((bf16[2,4,2,5120]{3,2,1,0:T(2,128)(2,1)}, bf16[2,4,2,5120]{3,2,1,0:T(2,128)(2,1)S(1)}, u32[]{:S(2)}, u32[]{:S(2)}) %collective-permute-start.1) | collective-permute-done | bytes 163872 | tf_op jit(solution)/shard_map/ppermute | solution.py:15
  13.8 29.4 %while.10 = (s32[]{:T(128)}, bf16[6,2,2,6400]{3,2,1,0:T(2,128)(2,1)S(1)}, bf16[2,2,5120]{2,1,0:T(2,128)(2,1)}, bf16[6,2,4,2,160]{4,3,2,1,0:T(2,128)(2,1)S(1)}, s...) while((s32[]{:T(128)}, ...), condition=%wide.region_4.5_spmd, body=%wide.region_0.4_spmd.sunk | while | flops 2490890 | bytes 6103269 | solution.py:92
  14.2 1.2 %reshape.219 = bf16[2,4,2,32,160]{4,3,2,1,0:T(8,128)(2,1)S(1)} reshape(bf16[2,4,2,5120]{3,2,1,0:T(2,128)(2,1)} %get-tuple-element.153) | data formatting | bytes 327680 | tf_op jit(solution)/shard_map/reshape.111
  17.9 0.6 multiply_reduce_fusion.5
  19.1 1.2 %reshape.219 = bf16[2,4,2,32,160]{4,3,2,1,0:T(8,128)(2,1)S(1)} reshape(bf16[2,4,2,5120]{3,2,1,0:T(2,128)(2,1)} %get-tuple-element.153) | data formatting | bytes 327680 | tf_op jit(solution)/shard_map/reshape.111
  22.8 0.6 multiply_reduce_fusion.5
  24.0 1.2 %reshape.219 = bf16[2,4,2,32,160]{4,3,2,1,0:T(8,128)(2,1)S(1)} reshape(bf16[2,4,2,5120]{3,2,1,0:T(2,128)(2,1)} %get-tuple-element.153) | data formatting | bytes 327680 | tf_op jit(solution)/shard_map/reshape.111
  27.7 0.6 multiply_reduce_fusion.5
  28.9 1.2 %reshape.219 = bf16[2,4,2,32,160]{4,3,2,1,0:T(8,128)(2,1)S(1)} reshape(bf16[2,4,2,5120]{3,2,1,0:T(2,128)(2,1)} %get-tuple-element.153) | data formatting | bytes 327680 | tf_op jit(solution)/shard_map/reshape.111
  32.6 0.6 multiply_reduce_fusion.5
  33.8 1.2 %reshape.219 = bf16[2,4,2,32,160]{4,3,2,1,0:T(8,128)(2,1)S(1)} reshape(bf16[2,4,2,5120]{3,2,1,0:T(2,128)(2,1)} %get-tuple-element.153) | data formatting | bytes 327680 | tf_op jit(solution)/shard_map/reshape.111
  37.5 0.6 multiply_reduce_fusion.5
  38.7 1.2 %reshape.219 = bf16[2,4,2,32,160]{4,3,2,1,0:T(8,128)(2,1)S(1)} reshape(bf16[2,4,2,5120]{3,2,1,0:T(2,128)(2,1)} %get-tuple-element.153) | data formatting | bytes 327680 | tf_op jit(solution)/shard_map/reshape.111
  42.4 0.6 multiply_reduce_fusion.5
  43.4 3.2 %collective-permute-start.2 = (bf16[2,1,2,6400]{3,2,0,1:T(2,128)(2,1)S(1)}, bf16[2,1,2,6400]{3,2,0,1:T(2,128)(2,1)S(1)}, u32[]{:S(2)}, u32[]{:S(2)}) collective-permute-start(bf16[2,1,2,6400]{3,2,0,1:T(2,128)(2,1)S(1)} %get-tuple-element.76), channel_id=1, source_target_pairs={{0,16},{16,32},{32,48},{48,64},{64,80},{80,96},{96,112},{112,128},... | collective-permute-start | bytes 153608 | tf_op jit(solution)/shard_map/ppermute | solution.py:12
  46.6 2.1 %collective-permute-start.3 = (bf16[2,1,2,6400]{3,2,0,1:T(2,128)(2,1)S(1)}, bf16[2,1,2,6400]{3,2,0,1:T(2,128)(2,1)S(1)}, u32[]{:S(2)}, u32[]{:S(2)}) collective-permute-start(bf16[2,1,2,6400]{3,2,0,1:T(2,128)(2,1)S(1)} %get-tuple-element.77), channel_id=1, source_target_pairs={{16,0},{32,16},{48,32},{64,48},{80,64},{96,80},{112,96},{128,112},... | collective-permute-start | bytes 153608 | tf_op jit(solution)/shard_map/ppermute | solution.py:15
  48.7 3.8 %collective-permute-done.3 = bf16[2,1,2,6400]{3,2,0,1:T(2,128)(2,1)S(1)} collective-permute-done((bf16[2,1,2,6400]{3,2,0,1:T(2,128)(2,1)S(1)}, bf16[2,1,2,6400]{3,2,0,1:T(2,128)(2,1)S(1)}, u32[]{:S(2)}, u32[]{:S(2)}) %collective-permute-start.3) | collective-permute-done | bytes 51232 | tf_op jit(solution)/shard_map/ppermute | solution.py:15
  52.5 0.6 pad_maximum_fusion.3
  53.1 0.6 fusion.239
  53.7 3.0 %collective-permute-start.4 = (bf16[2,8,1,6400]{3,2,0,1:T(2,128)(2,1)S(1)}, bf16[2,8,1,6400]{3,2,0,1:T(2,128)(2,1)S(1)}, u32[]{:S(2)}, u32[]{:S(2)}) collective-permute-start(bf16[2,8,1,6400]{3,2,0,1:T(2,128)(2,1)S(1)} %get-tuple-element.72), channel_id=1, source_target_pairs={{0,1},{1,2},{2,3},{3,4},{4,5},{5,6},{6,7},{7,8},{8,9},{9,10},{10,1... | collective-permute-start | bytes 614408 | tf_op jit(solution)/shard_map/ppermute | solution.py:12
  56.7 2.1 %collective-permute-start.5 = (bf16[2,8,1,6400]{3,2,0,1:T(2,128)(2,1)S(1)}, bf16[2,8,1,6400]{3,2,0,1:T(2,128)(2,1)S(1)}, u32[]{:S(2)}, u32[]{:S(2)}) collective-permute-start(bf16[2,8,1,6400]{3,2,0,1:T(2,128)(2,1)S(1)} %get-tuple-element.73), channel_id=1, source_target_pairs={{1,0},{2,1},{3,2},{4,3},{5,4},{6,5},{7,6},{8,7},{9,8},{10,9},{11,1... | collective-permute-start | bytes 614408 | tf_op jit(solution)/shard_map/ppermute | solution.py:15
  58.8 2.8 %collective-permute-done.4 = bf16[2,8,1,6400]{3,2,0,1:T(2,128)(2,1)S(1)} collective-permute-done((bf16[2,8,1,6400]{3,2,0,1:T(2,128)(2,1)S(1)}, bf16[2,8,1,6400]{3,2,0,1:T(2,128)(2,1)S(1)}, u32[]{:S(2)}, u32[]{:S(2)}) %collective-permute-start.4) | collective-permute-done | bytes 204832 | tf_op jit(solution)/shard_map/ppermute | solution.py:12
  61.6 5.6 %collective-permute-done.5 = bf16[2,8,1,6400]{3,2,0,1:T(2,128)(2,1)S(1)} collective-permute-done((bf16[2,8,1,6400]{3,2,0,1:T(2,128)(2,1)S(1)}, bf16[2,8,1,6400]{3,2,0,1:T(2,128)(2,1)S(1)}, u32[]{:S(2)}, u32[]{:S(2)}) %collective-permute-start.5) | collective-permute-done | bytes 204832 | tf_op jit(solution)/shard_map/ppermute | solution.py:15
  67.2 1.4 %pad_maximum_fusion.1 = bf16[2,8,4,6400]{3,2,0,1:T(4,128)(2,1)S(1)} fusion(bf16[2,8,1,6400]{3,2,0,1:T(2,128)(2,1)S(1)} %collective-permute-done.5, bf16[2,1,2,6400]{3,2,0,1:T(2,128)(2,1)S(1)} %collective-permute-done.3, bf16[2,6,2,6400]{3,2,0,1:T(2,128)(2,1)S(1)} %bitcast.511, bf16[2,1,2,6400]{3,2,0,1:T(2,128)(2,1)S(1)} %collective-permute-done.2, ...), kind=kLoop, calls=%fused_computation.93 | loop fusion | flops 4096000 | bytes 1638400 | tf_op jit(solution)/shard_map/concatenate | solution.py:16
  68.9 1.8 %reshape.151 = bf16[2,8,4,40,160]{4,3,2,1,0:T(8,128)(2,1)S(1)} reshape(bf16[2,8,4,6400]{3,2,1,0:T(4,128)(2,1)S(1)} %copy.11) | data formatting | bytes 1638400 | tf_op jit(solution)/shard_map/reshape | solution.py:49
  70.7 0.3 fusion.61
  71.0 0.3 fusion.63
  71.4 0.3 fusion.65
  71.7 0.3 fusion.57
  72.0 0.3 fusion.59
  72.4 0.3 fusion.53
  72.7 0.3 fusion.55
  73.1 0.3 fusion.49
  73.4 0.3 fusion.51
  73.8 0.3 fusion.45
  74.1 0.3 fusion.47
  74.5 0.3 convolution_bitcast_fusion.18
  74.8 0.3 convolution_bitcast_fusion.19
  75.2 0.3 convolution_bitcast_fusion.16
  75.5 0.3 convolution_bitcast_fusion.17
  75.9 0.3 convolution_bitcast_fusion.14
  76.2 0.3 convolution_bitcast_fusion.15
  76.6 0.3 convolution_bitcast_fusion.13
  79.3 0.4 copy-done.4
  79.9 0.6 reshape.152
  80.6 4.8 %collective-permute-start.6 = (bf16[2,1,2,5120]{3,2,1,0:T(2,128)(2,1)S(1)}, bf16[2,1,2,5120]{3,2,1,0:T(2,128)(2,1)S(1)}, u32[]{:S(2)}, u32[]{:S(2)}) collective-permute-start(bf16[2,1,2,5120]{3,2,1,0:T(2,128)(2,1)S(1)} %get-tuple-element.79), channel_id=1, source_target_pairs={{0,16},{16,32},{32,48},{48,64},{64,80},{80,96},{96,112},{112,128},... | collective-permute-start | bytes 122888 | tf_op jit(solution)/shard_map/ppermute | solution.py:12
  85.5 2.1 %collective-permute-start.7 = (bf16[2,1,2,5120]{3,2,1,0:T(2,128)(2,1)S(1)}, bf16[2,1,2,5120]{3,2,1,0:T(2,128)(2,1)S(1)}, u32[]{:S(2)}, u32[]{:S(2)}) collective-permute-start(bf16[2,1,2,5120]{3,2,1,0:T(2,128)(2,1)S(1)} %get-tuple-element.78), channel_id=1, source_target_pairs={{16,0},{32,16},{48,32},{64,48},{80,64},{96,80},{112,96},{128,112},... | collective-permute-start | bytes 122888 | tf_op jit(solution)/shard_map/ppermute | solution.py:15
  87.8 2.4 %collective-permute-done.7 = bf16[2,1,2,5120]{3,2,1,0:T(2,128)(2,1)S(1)} collective-permute-done((bf16[2,1,2,5120]{3,2,1,0:T(2,128)(2,1)S(1)}, bf16[2,1,2,5120]{3,2,1,0:T(2,128)(2,1)S(1)}, u32[]{:S(2)}, u32[]{:S(2)}) %collective-permute-start.7) | collective-permute-done | bytes 40992 | tf_op jit(solution)/shard_map/ppermute | solution.py:15
  90.2 0.5 fusion.240
  90.7 3.2 %collective-permute-start.8 = (bf16[2,8,1,5120]{3,2,1,0:T(2,128)(2,1)S(1)}, bf16[2,8,1,5120]{3,2,1,0:T(2,128)(2,1)S(1)}, u32[]{:S(2)}, u32[]{:S(2)}) collective-permute-start(bf16[2,8,1,5120]{3,2,1,0:T(2,128)(2,1)S(1)} %get-tuple-element.74), channel_id=1, source_target_pairs={{0,1},{1,2},{2,3},{3,4},{4,5},{5,6},{6,7},{7,8},{8,9},{9,10},{10,1... | collective-permute-start | bytes 491528 | tf_op jit(solution)/shard_map/ppermute | solution.py:12
  93.9 2.1 %collective-permute-start.9 = (bf16[2,8,1,5120]{3,2,1,0:T(2,128)(2,1)S(1)}, bf16[2,8,1,5120]{3,2,1,0:T(2,128)(2,1)S(1)}, u32[]{:S(2)}, u32[]{:S(2)}) collective-permute-start(bf16[2,8,1,5120]{3,2,1,0:T(2,128)(2,1)S(1)} %get-tuple-element.75), channel_id=1, source_target_pairs={{1,0},{2,1},{3,2},{4,3},{5,4},{6,5},{7,6},{8,7},{9,8},{10,9},{11,1... | collective-permute-start | bytes 491528 | tf_op jit(solution)/shard_map/ppermute | solution.py:15
  96.0 1.9 %collective-permute-done.8 = bf16[2,8,1,5120]{3,2,1,0:T(2,128)(2,1)S(1)} collective-permute-done((bf16[2,8,1,5120]{3,2,1,0:T(2,128)(2,1)S(1)}, bf16[2,8,1,5120]{3,2,1,0:T(2,128)(2,1)S(1)}, u32[]{:S(2)}, u32[]{:S(2)}) %collective-permute-start.8) | collective-permute-done | bytes 163872 | tf_op jit(solution)/shard_map/ppermute | solution.py:12
  97.9 5.8 %collective-permute-done.9 = bf16[2,8,1,5120]{3,2,1,0:T(2,128)(2,1)S(1)} collective-permute-done((bf16[2,8,1,5120]{3,2,1,0:T(2,128)(2,1)S(1)}, bf16[2,8,1,5120]{3,2,1,0:T(2,128)(2,1)S(1)}, u32[]{:S(2)}, u32[]{:S(2)}) %collective-permute-start.9) | collective-permute-done | bytes 163872 | tf_op jit(solution)/shard_map/ppermute | solution.py:15
  103.6 1.1 pad_maximum_fusion.2
  104.7 1.3 %reshape.153 = bf16[2,8,4,32,160]{4,3,2,1,0:T(8,128)(2,1)S(1)} reshape(bf16[2,8,4,5120]{3,2,1,0:T(4,128)(2,1)S(1)} %pad_maximum_fusion.2) | data formatting | bytes 1310720 | tf_op jit(solution)/shard_map/reshape | solution.py:49
  107.5 0.3 convolution_add_fusion.17
  109.4 0.3 convolution_add_fusion.11
  111.2 0.3 fusion.34
  114.0 0.4 copy-done.5
  114.7 1.3 %reshape.154 = bf16[2,6,2,5120]{3,2,1,0:T(2,128)(2,1)} reshape(bf16[2,6,2,32,160]{4,3,2,1,0:T(8,128)(2,1)S(1)} %fusion.36) | data formatting | bytes 491520 | tf_op jit(solution)/shard_map/reshape | solution.py:99
  (194 shorter events, 27.8 us)
Async XLA Ops:
  0.0 9.4 %collective-permute-start = (bf16[2,4,2,5120]{3,2,1,0:T(2,128)(2,1)}, bf16[2,4,2,5120]{3,2,1,0:T(2,128)(2,1)S(1)}, u32[]{:S(2)}, u32[]{:S(2)}) collective-permute-start(bf16[2,4,2,5120]{3,2,1,0:T(2,128)(2,1)} %param.11), channel_id=1, source_target_pairs={{0,1},{1,2},{2,3},{3,4},{4,5},{5,6},{6,7},{7,8},{8,9},{9,10},{10,1... | collective-permute-start | bytes 491528 | tf_op jit(solution)/shard_map/ppermute | solution.py:12
  5.8 8.1 %collective-permute-start.1 = (bf16[2,4,2,5120]{3,2,1,0:T(2,128)(2,1)}, bf16[2,4,2,5120]{3,2,1,0:T(2,128)(2,1)S(1)}, u32[]{:S(2)}, u32[]{:S(2)}) collective-permute-start(bf16[2,4,2,5120]{3,2,1,0:T(2,128)(2,1)} %param.11), channel_id=1, source_target_pairs={{1,0},{2,1},{3,2},{4,3},{5,4},{6,5},{7,6},{8,7},{9,8},{10,9},{11,1... | collective-permute-start | bytes 491528 | tf_op jit(solution)/shard_map/ppermute | solution.py:15
  13.8 2.4 %copy-start.1 = (bf16[2,2,5120]{2,1,0:T(2,128)(2,1)S(1)}, bf16[2,2,5120]{2,1,0:T(2,128)(2,1)}, u32[]{:S(2)}) copy-start(bf16[2,2,5120]{2,1,0:T(2,128)(2,1)} %get-tuple-element.149) | copy-start | bytes 122884 | tf_op jit(solution)/shard_map/while
  16.0 1.0 copy-start
  18.7 2.4 %copy-start.1 = (bf16[2,2,5120]{2,1,0:T(2,128)(2,1)S(1)}, bf16[2,2,5120]{2,1,0:T(2,128)(2,1)}, u32[]{:S(2)}) copy-start(bf16[2,2,5120]{2,1,0:T(2,128)(2,1)} %get-tuple-element.149) | copy-start | bytes 122884 | tf_op jit(solution)/shard_map/while
  20.9 1.0 copy-start
  23.6 2.4 %copy-start.1 = (bf16[2,2,5120]{2,1,0:T(2,128)(2,1)S(1)}, bf16[2,2,5120]{2,1,0:T(2,128)(2,1)}, u32[]{:S(2)}) copy-start(bf16[2,2,5120]{2,1,0:T(2,128)(2,1)} %get-tuple-element.149) | copy-start | bytes 122884 | tf_op jit(solution)/shard_map/while
  25.8 1.0 copy-start
  28.5 2.4 %copy-start.1 = (bf16[2,2,5120]{2,1,0:T(2,128)(2,1)S(1)}, bf16[2,2,5120]{2,1,0:T(2,128)(2,1)}, u32[]{:S(2)}) copy-start(bf16[2,2,5120]{2,1,0:T(2,128)(2,1)} %get-tuple-element.149) | copy-start | bytes 122884 | tf_op jit(solution)/shard_map/while
  30.8 1.0 copy-start
  33.5 2.4 %copy-start.1 = (bf16[2,2,5120]{2,1,0:T(2,128)(2,1)S(1)}, bf16[2,2,5120]{2,1,0:T(2,128)(2,1)}, u32[]{:S(2)}) copy-start(bf16[2,2,5120]{2,1,0:T(2,128)(2,1)} %get-tuple-element.149) | copy-start | bytes 122884 | tf_op jit(solution)/shard_map/while
  35.7 1.0 copy-start
  38.4 2.4 %copy-start.1 = (bf16[2,2,5120]{2,1,0:T(2,128)(2,1)S(1)}, bf16[2,2,5120]{2,1,0:T(2,128)(2,1)}, u32[]{:S(2)}) copy-start(bf16[2,2,5120]{2,1,0:T(2,128)(2,1)} %get-tuple-element.149) | copy-start | bytes 122884 | tf_op jit(solution)/shard_map/while
  40.6 1.0 copy-start
  43.4 5.3 %collective-permute-start.2 = (bf16[2,1,2,6400]{3,2,0,1:T(2,128)(2,1)S(1)}, bf16[2,1,2,6400]{3,2,0,1:T(2,128)(2,1)S(1)}, u32[]{:S(2)}, u32[]{:S(2)}) collective-permute-start(bf16[2,1,2,6400]{3,2,0,1:T(2,128)(2,1)S(1)} %get-tuple-element.76), channel_id=1, source_target_pairs={{0,16},{16,32},{32,48},{48,64},{64,80},{80,96},{96,112},{112,128},... | collective-permute-start | bytes 153608 | tf_op jit(solution)/shard_map/ppermute | solution.py:12
  46.6 5.9 %collective-permute-start.3 = (bf16[2,1,2,6400]{3,2,0,1:T(2,128)(2,1)S(1)}, bf16[2,1,2,6400]{3,2,0,1:T(2,128)(2,1)S(1)}, u32[]{:S(2)}, u32[]{:S(2)}) collective-permute-start(bf16[2,1,2,6400]{3,2,0,1:T(2,128)(2,1)S(1)} %get-tuple-element.77), channel_id=1, source_target_pairs={{16,0},{32,16},{48,32},{64,48},{80,64},{96,80},{112,96},{128,112},... | collective-permute-start | bytes 153608 | tf_op jit(solution)/shard_map/ppermute | solution.py:15
  53.7 7.9 %collective-permute-start.4 = (bf16[2,8,1,6400]{3,2,0,1:T(2,128)(2,1)S(1)}, bf16[2,8,1,6400]{3,2,0,1:T(2,128)(2,1)S(1)}, u32[]{:S(2)}, u32[]{:S(2)}) collective-permute-start(bf16[2,8,1,6400]{3,2,0,1:T(2,128)(2,1)S(1)} %get-tuple-element.72), channel_id=1, source_target_pairs={{0,1},{1,2},{2,3},{3,4},{4,5},{5,6},{6,7},{7,8},{8,9},{9,10},{10,1... | collective-permute-start | bytes 614408 | tf_op jit(solution)/shard_map/ppermute | solution.py:12
  56.7 10.5 %collective-permute-start.5 = (bf16[2,8,1,6400]{3,2,0,1:T(2,128)(2,1)S(1)}, bf16[2,8,1,6400]{3,2,0,1:T(2,128)(2,1)S(1)}, u32[]{:S(2)}, u32[]{:S(2)}) collective-permute-start(bf16[2,8,1,6400]{3,2,0,1:T(2,128)(2,1)S(1)} %get-tuple-element.73), channel_id=1, source_target_pairs={{1,0},{2,1},{3,2},{4,3},{5,4},{6,5},{7,6},{8,7},{9,8},{10,9},{11,1... | collective-permute-start | bytes 614408 | tf_op jit(solution)/shard_map/ppermute | solution.py:15
  68.8 1.8 %copy-start.2 = (bf16[3,3,3,32,40]{4,3,2,1,0:T(8,128)(2,1)S(1)}, bf16[3,3,3,32,40]{4,3,2,1,0:T(8,128)(2,1)}, u32[]{:S(2)}) copy-start(bf16[3,3,3,32,40]{4,3,2,1,0:T(8,128)(2,1)} %param.14) | copy-start | bytes 207364
  79.0 0.7 copy-start.4
  80.6 7.0 %collective-permute-start.6 = (bf16[2,1,2,5120]{3,2,1,0:T(2,128)(2,1)S(1)}, bf16[2,1,2,5120]{3,2,1,0:T(2,128)(2,1)S(1)}, u32[]{:S(2)}, u32[]{:S(2)}) collective-permute-start(bf16[2,1,2,5120]{3,2,1,0:T(2,128)(2,1)S(1)} %get-tuple-element.79), channel_id=1, source_target_pairs={{0,16},{16,32},{32,48},{48,64},{64,80},{80,96},{96,112},{112,128},... | collective-permute-start | bytes 122888 | tf_op jit(solution)/shard_map/ppermute | solution.py:12
  85.5 4.7 %collective-permute-start.7 = (bf16[2,1,2,5120]{3,2,1,0:T(2,128)(2,1)S(1)}, bf16[2,1,2,5120]{3,2,1,0:T(2,128)(2,1)S(1)}, u32[]{:S(2)}, u32[]{:S(2)}) collective-permute-start(bf16[2,1,2,5120]{3,2,1,0:T(2,128)(2,1)S(1)} %get-tuple-element.78), channel_id=1, source_target_pairs={{16,0},{32,16},{48,32},{64,48},{80,64},{96,80},{112,96},{128,112},... | collective-permute-start | bytes 122888 | tf_op jit(solution)/shard_map/ppermute | solution.py:15
  90.7 7.2 %collective-permute-start.8 = (bf16[2,8,1,5120]{3,2,1,0:T(2,128)(2,1)S(1)}, bf16[2,8,1,5120]{3,2,1,0:T(2,128)(2,1)S(1)}, u32[]{:S(2)}, u32[]{:S(2)}) collective-permute-start(bf16[2,8,1,5120]{3,2,1,0:T(2,128)(2,1)S(1)} %get-tuple-element.74), channel_id=1, source_target_pairs={{0,1},{1,2},{2,3},{3,4},{4,5},{5,6},{6,7},{7,8},{8,9},{9,10},{10,1... | collective-permute-start | bytes 491528 | tf_op jit(solution)/shard_map/ppermute | solution.py:12
  93.9 12.2 %copy-start.3 = (bf16[3,3,3,32,32]{4,3,2,1,0:T(8,128)(2,1)S(1)}, bf16[3,3,3,32,32]{4,3,2,1,0:T(8,128)(2,1)}, u32[]{:S(2)}) copy-start(bf16[3,3,3,32,32]{4,3,2,1,0:T(8,128)(2,1)} %param.16) | copy-start | bytes 165892
  93.9 9.7 %collective-permute-start.9 = (bf16[2,8,1,5120]{3,2,1,0:T(2,128)(2,1)S(1)}, bf16[2,8,1,5120]{3,2,1,0:T(2,128)(2,1)S(1)}, u32[]{:S(2)}, u32[]{:S(2)}) collective-permute-start(bf16[2,8,1,5120]{3,2,1,0:T(2,128)(2,1)S(1)} %get-tuple-element.75), channel_id=1, source_target_pairs={{1,0},{2,1},{3,2},{4,3},{5,4},{6,5},{7,6},{8,7},{9,8},{10,9},{11,1... | collective-permute-start | bytes 491528 | tf_op jit(solution)/shard_map/ppermute | solution.py:15
  113.7 0.7 copy-start.5
where the time goes:
time: 117 us; the launch traced here: 116 us
  starting transfers between devices  30.3 us (26%)
  local copies, waits for them, and re-layouts  28.5 us (24%)
  waiting for transfers between devices  26.7 us (23%)
  matrix products  16.8 us (14%)
  other arithmetic  12 us (10%)
    ppermute x5, waiting for transfers between devices, extended(): lax.ppermute(lax.slice_in_dim(block, 0, width, axis=dim), axis, backward)  22 us
    ppermute x5, starting transfers between devices, extended(): lax.ppermute(lax.slice_in_dim(block, block.shape[dim] - width, None, axis...  20 us
    dot_general x54, matrix products, convolve(): jnp.einsum('bprcw,oc->bprow', piece, kernel[tap_depth, tap_row, tap_col],...  16.8 us
    another operation x36, local copies, waits for them, and re-layouts  15.6 us
    ppermute x5, starting transfers between devices, extended(): lax.ppermute(lax.slice_in_dim(block, 0, width, axis=dim), axis, backward)  10.3 us
    ppermute x5, waiting for transfers between devices, extended(): lax.ppermute(lax.slice_in_dim(block, block.shape[dim] - width, None, axis...  4.7 us
    reduce_sum x6, other arithmetic, cost_plane(): jnp.sum(products, axis=(1, 4)) / (source_views * per_group * 1.0)  3.56 us
    concatenate x3, other arithmetic, extended(): block = jnp.concatenate([low, block, high], axis=dim)  3.1 us
  transfers between devices with their start and end apart: 10, of which 7 were waited for; matrix products, arithmetic and copies ran while one was open for 2% of the time, Pallas kernels for 0%

commit v1 on v0

v1 whole, which is shorter than its diff:
```python
import functools

import jax
import jax.numpy as jnp
from jax import lax
from jax.experimental import pallas as pl
from jax.experimental.pallas import tpu as pltpu
from jax.sharding import PartitionSpec as P

F32 = jnp.float32
BF16 = jnp.bfloat16


def pack_features(rows, groups, per_group, columns):
    b, v, m, _ = rows.shape
    x = rows.reshape(b, v, m, groups, per_group, columns)
    return x.transpose(1, 4, 3, 0, 2, 5).reshape(v * per_group * groups, b * m * columns)


def pack_blend(weight):
    b, v, p, m, w = weight.shape
    return weight.transpose(2, 1, 0, 3, 4).reshape(p * v, b * m * w)


def compute_kernel(
    own_ref, halo_ref, w1_ref, w2_ref, b1_ref, b2_ref, out_ref,
    src_ref, rf_ref, tm_ref, tp_ref, e0_ref, dm_ref, dp_ref, vf_ref, v_ref, h_ref,
    *, planes, columns, depth_count, row_count,
):
    q = lax.axis_index("rows")
    core = q % 2
    depth = lax.axis_index("depth")
    lanes = 4 * columns
    views = 4
    first = depth == 0
    last = depth == depth_count - 1

    lane = lax.broadcasted_iota(jnp.int32, (1, lanes), 1)
    col = lane % columns
    row_bit = (lane // columns) % 2

    for i in range(2):
        src_ref[i] = halo_ref[0, 128 * i : 128 * i + 128, :]
        src_ref[2 + i] = own_ref[i, 0:128, :]
        src_ref[4 + i] = halo_ref[1, 128 * i : 128 * i + 128, :]
    half = lax.broadcasted_iota(jnp.int32, (8, 128), 1) < 64

    def put_weights(r, row, w, o):
        turned = pltpu.roll(o, 64, 1)
        b0 = jnp.where(half, o, turned)
        b1 = jnp.where(half, turned, o)
        below = jnp.concatenate([b0, b0, o, b1, b1], axis=1) < -0.5
        tm_ref[r, row : row + 8, :] = jnp.where(below, w, 0.0)
        tp_ref[r, row : row + 8, :] = jnp.where(below, 0.0, 1.0 - w)

    for r in range(4):
        if r == 0:
            rest = halo_ref[0, 256:320, :]
        elif r == 3:
            rest = halo_ref[1, 256:320, :]
        else:
            rest = own_ref[r - 1, 128:192, :]
        rest = rest.astype(F32)
        rf_ref[r] = rest[0:32]
        for i in range(planes * views // 8):
            put_weights(r, 8 + 8 * i, rest[32 + 8 * i : 40 + 8 * i], rest[56:64, 128 * i : 128 * i + 128])
        low_row = (352, 320, 336, 368)[r]
        high_row = (368, 320, 336, 352)[r]
        low = halo_ref[0, low_row : low_row + 16, :].astype(F32)
        high = halo_ref[1, high_row : high_row + 16, :].astype(F32)
        put_weights(r, 0, low[0:8], low[8:16, 0:128])
        put_weights(r, 8 + planes * views, high[0:8], high[8:16, 0:128])

    for k in range(3):
        base = rf_ref[core + k]
        for v in range(views):
            rows = slice(32 * v, 32 * v + 32)
            middle = src_ref[core + k + 1, rows, :].astype(F32)
            e0_ref[k, v] = middle - base
            dm_ref[k, v] = src_ref[core + k, rows, :].astype(F32) - middle
            dp_ref[k, v] = src_ref[core + k + 2, rows, :].astype(F32) - middle

    def volume_plane(pair, carry):
        outside = ((pair == 0) & first) | ((pair == planes // 2 + 1) & last)
        row = pl.multiple_of(pair * 8, 8)
        for k in range(3):
            missing = outside | ((k == 0) & (q == 0)) | ((k == 2) & (q == row_count - 1))
            keep = jnp.where(missing, 0.0, 1.0).astype(F32)
            for i in range(lanes // 128):
                cols = slice(128 * i, 128 * i + 128)
                tm = tm_ref[core + k, pl.ds(row, 8), cols]
                tp = tp_ref[core + k, pl.ds(row, 8), cols]
                base = rf_ref[core + k, :, cols]
                for t in range(2):
                    total = jnp.zeros((32, 128), F32)
                    squares = jnp.zeros((32, 128), F32)
                    for v in range(views):
                        n = views * t + v
                        e = e0_ref[k, v, :, cols] + tm[n : n + 1] * dm_ref[k, v, :, cols]
                        e = e + tp[n : n + 1] * dp_ref[k, v, :, cols]
                        total = total + e
                        squares = squares + e * e
                    spread = squares * (0.2 * keep) - total * total * (0.04 * keep)
                    product = base * (total + 4.0 * base)
                    corr = (product[0:8] + product[8:16] + product[16:24] + product[24:32]) * keep
                    vf_ref[t, k, 0:32, cols] = spread
                    vf_ref[t, k, 32:40, cols] = corr
        for t in range(2):
            p = 2 * pair + t
            for k in range(3):
                v_ref[p, 96 * k : 96 * k + 48, :] = vf_ref[t, k].astype(BF16)
            for k in range(2):
                mixed = jnp.where(
                    row_bit == 0,
                    pltpu.roll(vf_ref[t, k], lanes - columns, 1),
                    pltpu.roll(vf_ref[t, k + 1], columns, 1),
                )
                v_ref[p, 96 * k + 48 : 96 * k + 96, :] = mixed.astype(BF16)
        return carry

    vf_ref[:, :, 40:48, :] = jnp.zeros((2, 3, 8, lanes), F32)
    lax.fori_loop(0, planes // 2 + 2, volume_plane, 0)

    def shifted_sum(parts, width):
        column = jnp.concatenate([col] * (width // lanes), axis=1)
        left = jnp.where(column == 0, 0.0, pltpu.roll(parts[0:32], 1, 1))
        right = jnp.where(column == columns - 1, 0.0, pltpu.roll(parts[64:96], width - 1, 1))
        return parts[32:64] + left + right

    lost = jnp.concatenate(
        [
            jnp.where((row_bit == 0) & (q == 0), 0.0, 1.0),
            jnp.where((row_bit == 1) & (q == row_count - 1), 0.0, 1.0),
        ],
        axis=1,
    )

    def hidden_plane(p, carry):
        upper = jnp.concatenate([v_ref[p + a, 0:144, :] for a in range(3)], axis=0)
        lower = jnp.concatenate([v_ref[p + a, 96:240, :] for a in range(3)], axis=0)
        taps = jnp.concatenate([upper, lower], axis=1)
        parts = jnp.dot(w1_ref[...], taps, preferred_element_type=F32)
        missing = ((p == 0) & first) | ((p == planes + 1) & last)
        keep = lost * jnp.where(missing, 0.0, 1.0).astype(F32)
        hidden = jnp.maximum(shifted_sum(parts, 2 * lanes) + b1_ref[...], 0.0) * keep
        above = hidden[:, :lanes]
        below = hidden[:, lanes:]
        h_ref[p, 0:32, :] = above.astype(BF16)
        h_ref[p, 64:96, :] = below.astype(BF16)
        mixed = jnp.where(row_bit == 0, pltpu.roll(above, lanes - columns, 1), pltpu.roll(below, columns, 1))
        h_ref[p, 32:64, :] = mixed.astype(BF16)
        return carry

    lax.fori_loop(0, planes + 2, hidden_plane, 0)

    def out_plane(p, carry):
        taps = jnp.concatenate([h_ref[p + a] for a in range(3)], axis=0)
        parts = jnp.dot(w2_ref[...], taps, preferred_element_type=F32)
        out_ref[p] = (shifted_sum(parts, lanes) + b2_ref[...]).astype(BF16)
        return carry

    lax.fori_loop(0, planes, out_plane, 0)


def body(ref_feat, src_feat, block_index, blend, conv_first, bias_first, conv_second, bias_second):
    b, v, m, packed = src_feat.shape
    planes, columns = blend.shape[2], blend.shape[4]
    channels = conv_first.shape[4]
    outputs = conv_first.shape[3]
    feat = packed // columns
    groups = channels - feat
    per_group = feat // groups
    depth_count = lax.axis_size("depth")
    row_count = lax.axis_size("rows")
    lanes = b * m * columns
    core = lax.axis_index("rows") % 2

    offset = (block_index[:, :, :, 0] - lax.axis_index("rows")).astype(BF16)
    offset = offset.transpose(2, 1, 0).reshape(planes * v // 8, 8, b, 1)
    offset = jnp.broadcast_to(offset, (planes * v // 8, 8, b, 64)).transpose(1, 0, 2, 3).reshape(8, -1)
    offset = jnp.pad(offset, ((0, 0), (0, lanes - offset.shape[1])))
    own = jnp.concatenate(
        [
            pack_features(src_feat, groups, per_group, columns),
            pack_features(ref_feat[:, None], groups, per_group, columns),
            pack_blend(blend),
            offset,
        ],
        axis=0,
    )
    pairs = [[2 * i, 2 * i + 1] for i in range(row_count // 2)]
    gathered = lax.all_gather(own, "rows", axis_index_groups=pairs)

    def send(x, step_depth, step_chip):
        routes = []
        for d in range(depth_count):
            for r in range(row_count):
                sign = 1 if r % 2 == 0 else -1
                to_d, to_r = d + sign * step_depth, r + 2 * sign * step_chip
                if 0 <= to_d < depth_count and 0 <= to_r < row_count:
                    routes.append((d * row_count + r, to_d * row_count + to_r))
        return lax.ppermute(x, ("depth", "rows"), routes)

    edge_offset = jnp.where(core == 0, gathered[:, 184:192, 256:384], gathered[:, 184:192, 0:128])
    edge_blend = jnp.where(core == 0, gathered[:, 176:184], gathered[:, 160:168])
    edge = jnp.concatenate([edge_blend, jnp.pad(edge_offset, ((0, 0), (0, 0), (0, lanes - 128)))], axis=1)
    from_chip = send(gathered, 0, 1)
    from_depth = send(edge, 1, 0)
    from_same = send(edge, 1, 1)
    from_cross = send(edge, 1, -1)
    halo = jnp.concatenate(
        [
            from_chip[0, 0:128],
            from_chip[1, 0:128],
            lax.dynamic_index_in_dim(from_chip, 1 - core, 0, keepdims=False)[128:192],
            from_depth[0],
            from_depth[1],
            lax.dynamic_index_in_dim(from_same, 1 - core, 0, keepdims=False),
            lax.dynamic_index_in_dim(from_cross, core, 0, keepdims=False),
        ],
        axis=0,
    )
    halos = lax.all_gather(halo, "rows", axis_index_groups=pairs)

    corr = conv_first[..., :groups] * jnp.asarray(0.0625, BF16)
    spread = conv_first[..., groups:].reshape(3, 3, 3, outputs, groups, per_group)
    spread = spread.swapaxes(4, 5).reshape(3, 3, 3, outputs, feat)
    padded = jnp.concatenate([spread, corr, jnp.zeros_like(corr)], axis=-1)
    w1 = padded.transpose(2, 3, 0, 1, 4).reshape(3 * outputs, -1)
    w2 = conv_second.transpose(2, 3, 0, 1, 4).reshape(3 * outputs, -1)

    kernel = functools.partial(
        compute_kernel, planes=planes, columns=columns, depth_count=depth_count, row_count=row_count
    )
    out = pl.pallas_call(
        kernel,
        out_shape=jax.ShapeDtypeStruct((planes, outputs, lanes), BF16),
        in_specs=[pl.BlockSpec(memory_space=pltpu.VMEM)] * 6,
        out_specs=pl.BlockSpec(memory_space=pltpu.VMEM),
        scratch_shapes=[
            pltpu.VMEM((6, 128, lanes), BF16),
            pltpu.VMEM((4, 32, lanes), F32),
            pltpu.VMEM((4, (planes + 4) * v, lanes), F32),
            pltpu.VMEM((4, (planes + 4) * v, lanes), F32),
            pltpu.VMEM((3, v, 32, lanes), F32),
            pltpu.VMEM((3, v, 32, lanes), F32),
            pltpu.VMEM((3, v, 32, lanes), F32),
            pltpu.VMEM((2, 3, 48, lanes), F32),
            pltpu.VMEM((planes + 4, 240, lanes), BF16),
            pltpu.VMEM((planes + 2, 96, lanes), BF16),
        ],
        compiler_params=pltpu.CompilerParams(vmem_limit_bytes=48 * 1024 * 1024),
        name="volume_and_convolutions",
    )(gathered, halos, w1, w2, bias_first[:, None], bias_second[:, None])
    out = out.reshape(planes, outputs, b, m, columns).transpose(2, 0, 3, 1, 4)
    return out.reshape(b, planes, m, outputs * columns)


def solution(mesh):
    in_specs = (
        P(None, "rows", None),
        P(None, None, "rows", None),
        P(None, None, "depth", "rows"),
        P(None, None, "depth", "rows", None),
        P(),
        P(),
        P(),
        P(),
    )
    out_specs = P(None, "depth", "rows", None)
    return jax.shard_map(body, mesh=mesh, in_specs=in_specs, out_specs=out_specs, check_vma=False)
```

time: 117 us -> 45 us (0.38)
  the two profiles are of different devices: /device:TPU:215 before, /device:TPU:199 now
where the time goes in v1:
time: 45 us; the launch traced here: 44.6 us
  starting transfers between devices  15.3 us (34%)
  local copies, waits for them, and re-layouts  9.83 us (22%)
  Pallas kernels  9.6 us (21%)
  blocking collectives  9.31 us (21%)
    ppermute x4, starting transfers between devices, send(): return lax.ppermute(x, ('depth', 'rows'), routes)  15.3 us
    pallas_call x1, Pallas kernels, body(): pl.pallas_call(kernel, out_shape=jax.ShapeDtypeStruct((planes, outputs, l...  9.6 us
    all_gather x1, blocking collectives, body(): halos = lax.all_gather(halo, 'rows', axis_index_groups=pairs)  6.72 us
    unnamed x23, local copies, waits for them, and re-layouts  4.39 us
    all_gather x1, blocking collectives, body(): gathered = lax.all_gather(own, 'rows', axis_index_groups=pairs)  2.59 us
    reshape x1, local copies, waits for them, and re-layouts, body(): return out.reshape(b, planes, m, outputs * columns)  1.31 us
    reshape x1, local copies, waits for them, and re-layouts, pack_features(): x = rows.reshape(b, v, m, groups, per_group, columns)  1.18 us
  transfers between devices with their start and end apart: 4, of which 0 were waited for; matrix products, arithmetic and copies ran while one was open for 4% of the time, Pallas kernels for 0%

profile of v1, /device:TPU:199, one launch (start us, length us, event | category | flops | bytes accessed | tf_op | source)
XLA Modules:
  0.0 44.6 jit_solution(14605158536041175832)
XLA Ops:
  0.0 0.0 copy-start.4
  0.0 0.7 %copy-done.4 = s32[2,4,6,1]{2,3,1,0:T(1,128)S(1)} copy-done((s32[2,4,6,1]{2,3,1,0:T(1,128)S(1)}, s32[2,4,6,1]{2,3,1,0:T(1,128)}, u32[]{:S(2)}) %copy-start.4) | copy-done | bytes 216
  0.7 0.1 copy.22
  0.8 0.1 broadcast_in_dim.16
  0.9 0.1 copy.23
  1.0 0.1 broadcast_bitcast_fusion
  1.1 0.1 reshape.43
  1.2 1.2 %reshape.39 = bf16[2,4,2,8,4,160]{5,4,3,2,1,0:T(4,128)(2,1)S(1)} reshape(bf16[2,4,2,5120]{3,2,1,0:T(2,128)(2,1)} %param.9) | data formatting | bytes 327680 | tf_op jit(solution)/shard_map/reshape | solution.py:16
  2.4 0.3 copy.19
  2.7 0.0 copy-start.3
  2.7 0.2 reshape.40
  2.9 0.6 %copy-done.3 = bf16[2,2,5120]{2,1,0:T(2,128)(2,1)S(1)} copy-done((bf16[2,2,5120]{2,1,0:T(2,128)(2,1)S(1)}, bf16[2,2,5120]{2,1,0:T(2,128)(2,1)}, u32[]{:S(2)}) %copy-start.3) | copy-done | bytes 40984
  3.5 0.1 reshape_broadcast_in_dim.3
  3.6 0.1 copy.20
  3.7 0.0 copy-start.2
  3.7 0.1 reshape.41
  3.8 0.7 %copy-done.2 = bf16[2,4,6,2,160]{4,3,2,1,0:T(2,128)(2,1)S(1)} copy-done((bf16[2,4,6,2,160]{4,3,2,1,0:T(2,128)(2,1)S(1)}, bf16[2,4,6,2,160]{4,3,2,1,0:T(2,128)(2,1)}, u32[]{:S(2)}) %copy-start.2) | copy-done | bytes 30744
  4.5 0.1 reshape.42
  4.6 0.0 copy-start
  4.6 2.6 %all-gather = bf16[384,640]{1,0:T(8,128)(2,1)S(1)} all-gather(bf16[192,640]{1,0:T(8,128)(2,1)S(1)} %fusion.1), channel_id=2, replica_groups={{0,1},{2,3},{4,5},{6,7},{8,9},{10,11},{12,13},{14,15},{16,17},{18,19},{..., dimensions={0}, use_global_device_ids=true | all-gather | bytes 737280 | tf_op jit(solution)/shard_map/all_gather | solution.py:192
  7.2 1.9 %collective-permute-start = (bf16[2,192,640]{2,1,0:T(8,128)(2,1)S(1)}, bf16[2,192,640]{2,1,0:T(8,128)(2,1)S(1)}, u32[]{:S(2)}, u32[]{:S(2)}) collective-permute-start(bf16[2,192,640]{2,1,0:T(8,128)(2,1)S(1)} %bitcast.54), channel_id=1, source_target_pairs={{0,2},{2,4},{3,1},{4,6},{5,3},{6,8},{7,5},{8,10},{9,7},{10,12},{11... | collective-permute-start | bytes 1474568 | tf_op jit(solution)/shard_map/ppermute | solution.py:202
  9.2 5.4 %collective-permute-start.1 = (bf16[2,16,640]{2,1,0:T(8,128)(2,1)S(1)}, bf16[2,16,640]{2,1,0:T(8,128)(2,1)S(1)}, u32[]{:S(2)}, u32[]{:S(2)}) collective-permute-start(bf16[2,16,640]{2,1,0:T(8,128)(2,1)S(1)} %fusion.6), channel_id=1, source_target_pairs={{0,16},{2,18},{4,20},{6,22},{8,24},{10,26},{12,28},{14,30},{16,32}... | collective-permute-start | bytes 122888 | tf_op jit(solution)/shard_map/ppermute | solution.py:202
  14.6 2.1 %collective-permute-start.2 = (bf16[2,16,640]{2,1,0:T(8,128)(2,1)S(1)}, bf16[2,16,640]{2,1,0:T(8,128)(2,1)S(1)}, u32[]{:S(2)}, u32[]{:S(2)}) collective-permute-start(bf16[2,16,640]{2,1,0:T(8,128)(2,1)S(1)} %fusion.6), channel_id=1, source_target_pairs={{0,18},{2,20},{4,22},{6,24},{8,26},{10,28},{12,30},{16,34},{18,36}... | collective-permute-start | bytes 122888 | tf_op jit(solution)/shard_map/ppermute | solution.py:202
  16.7 6.0 %collective-permute-start.3 = (bf16[2,16,640]{2,1,0:T(8,128)(2,1)S(1)}, bf16[2,16,640]{2,1,0:T(8,128)(2,1)S(1)}, u32[]{:S(2)}, u32[]{:S(2)}) collective-permute-start(bf16[2,16,640]{2,1,0:T(8,128)(2,1)S(1)} %fusion.6), channel_id=1, source_target_pairs={{2,16},{4,18},{6,20},{8,22},{10,24},{12,26},{14,28},{17,3},{18,32}... | collective-permute-start | bytes 122888 | tf_op jit(solution)/shard_map/ppermute | solution.py:202
  22.7 0.0 copy-done
  22.7 0.1 slice.46
  22.8 0.2 copy.33
  23.0 0.1 copy.34
  23.2 0.1 pad.12.clone
  23.3 0.1 maximum_bitcast_fusion
  23.4 0.2 copy.27
  23.6 0.0 copy-start.1
  23.6 0.2 reshape.46.w1_ref
  23.8 0.7 %copy-done.1 = bf16[3,3,3,32,32]{4,3,2,1,0:T(8,128)(2,1)S(1)} copy-done((bf16[3,3,3,32,32]{4,3,2,1,0:T(8,128)(2,1)S(1)}, bf16[3,3,3,32,32]{4,3,2,1,0:T(8,128)(2,1)}, u32[]{:S(2)}) %copy-start.1) | copy-done | bytes 55320
  24.6 0.2 copy.28
  24.7 0.2 reshape.47.w2_ref
  24.9 0.0 copy-start.5
  24.9 0.6 %copy-done.5 = f32[32]{0:T(128)S(1)} copy-done((f32[32]{0:T(128)S(1)}, f32[32]{0:T(128)}, u32[]{:S(2)}) %copy-start.5) | copy-done | bytes 152
  25.6 0.1 copy.29.b1_ref
  25.6 0.0 copy-start.6
  25.7 0.7 %copy-done.6 = f32[32]{0:T(128)S(1)} copy-done((f32[32]{0:T(128)S(1)}, f32[32]{0:T(128)}, u32[]{:S(2)}) %copy-start.6) | copy-done | bytes 152
  26.3 0.1 copy.30.b2_ref
  26.4 0.0 collective-permute-done
  26.5 0.0 collective-permute-done.1
  26.5 0.0 collective-permute-done.2
  26.5 0.0 collective-permute-done.3
  26.6 6.7 %all-gather.1 = bf16[768,640]{1,0:T(8,128)(2,1)S(1)} all-gather(bf16[384,640]{1,0:T(8,128)(2,1)S(1)} %bitcast_dynamic-update-slice_fusion), channel_id=3, replica_groups={{0,1},{2,3},{4,5},{6,7},{8,9},{10,11},{12,13},{14,15},{16,17},{18,19},{..., dimensions={0}, use_global_device_ids=true | all-gather | bytes 1474560 | tf_op jit(solution)/shard_map/all_gather | solution.py:223
  33.3 9.6 %volume_and_convolutions.1 = bf16[6,32,640]{2,1,0:T(8,128)(2,1)S(1)} custom-call(bf16[2,192,640]{2,1,0:T(8,128)(2,1)S(1)} %bitcast.57, bf16[2,384,640]{2,1,0:T(8,128)(2,1)S(1)} %bitcast.53, bf16[96,432]{1,0:T(8,128)(2,1)S(1)} %reshape.46.w1_ref, bf16[96,288]{1,0:T(8,128)(2,1)S(1)} %reshape.47.w2_ref, f32[32,1]{1,0:T(8,128)S(1)} %copy.29.b1_ref, ...), custom_call_target="tpu_custom_call" | custom-call | tf_op jit(solution)/shard_map/volume_and_convolutions/pallas_call | solution.py:235
  42.9 0.3 reshape.48
  43.2 0.1 copy.31
  43.3 1.3 %reshape.49 = bf16[2,6,2,5120]{3,2,1,0:T(2,128)(2,1)} reshape(bf16[2,6,2,32,160]{4,3,2,1,0:T(8,128)(2,1)S(1)} %copy.31) | data formatting | bytes 491520 | tf_op jit(solution)/shard_map/reshape | solution.py:256
  (17 shorter events, 0.3 us)
Async XLA Ops:
  0.0 0.7 %copy-start.4 = (s32[2,4,6,1]{2,3,1,0:T(1,128)S(1)}, s32[2,4,6,1]{2,3,1,0:T(1,128)}, u32[]{:S(2)}) copy-start(s32[2,4,6,1]{2,3,1,0:T(1,128)} %param.10) | copy-start | bytes 580
  2.7 0.8 %copy-start.3 = (bf16[2,2,5120]{2,1,0:T(2,128)(2,1)S(1)}, bf16[2,2,5120]{2,1,0:T(2,128)(2,1)}, u32[]{:S(2)}) copy-start(bf16[2,2,5120]{2,1,0:T(2,128)(2,1)} %param.8) | copy-start | bytes 122884
  3.7 0.8 %copy-start.2 = (bf16[2,4,6,2,160]{4,3,2,1,0:T(2,128)(2,1)S(1)}, bf16[2,4,6,2,160]{4,3,2,1,0:T(2,128)(2,1)}, u32[]{:S(2)}) copy-start(bf16[2,4,6,2,160]{4,3,2,1,0:T(2,128)(2,1)} %param.11) | copy-start | bytes 92164
  4.6 18.0 %copy-start = (bf16[3,3,3,32,40]{4,3,2,1,0:T(8,128)(2,1)S(1)}, bf16[3,3,3,32,40]{4,3,2,1,0:T(8,128)(2,1)}, u32[]{:S(2)}) copy-start(bf16[3,3,3,32,40]{4,3,2,1,0:T(8,128)(2,1)} %param.12) | copy-start | bytes 207364
  7.2 19.2 %collective-permute-start = (bf16[2,192,640]{2,1,0:T(8,128)(2,1)S(1)}, bf16[2,192,640]{2,1,0:T(8,128)(2,1)S(1)}, u32[]{:S(2)}, u32[]{:S(2)}) collective-permute-start(bf16[2,192,640]{2,1,0:T(8,128)(2,1)S(1)} %bitcast.54), channel_id=1, source_target_pairs={{0,2},{2,4},{3,1},{4,6},{5,3},{6,8},{7,5},{8,10},{9,7},{10,12},{11... | collective-permute-start | bytes 1474568 | tf_op jit(solution)/shard_map/ppermute | solution.py:202
  9.2 17.3 %collective-permute-start.1 = (bf16[2,16,640]{2,1,0:T(8,128)(2,1)S(1)}, bf16[2,16,640]{2,1,0:T(8,128)(2,1)S(1)}, u32[]{:S(2)}, u32[]{:S(2)}) collective-permute-start(bf16[2,16,640]{2,1,0:T(8,128)(2,1)S(1)} %fusion.6), channel_id=1, source_target_pairs={{0,16},{2,18},{4,20},{6,22},{8,24},{10,26},{12,28},{14,30},{16,32}... | collective-permute-start | bytes 122888 | tf_op jit(solution)/shard_map/ppermute | solution.py:202
  14.6 11.9 %collective-permute-start.2 = (bf16[2,16,640]{2,1,0:T(8,128)(2,1)S(1)}, bf16[2,16,640]{2,1,0:T(8,128)(2,1)S(1)}, u32[]{:S(2)}, u32[]{:S(2)}) collective-permute-start(bf16[2,16,640]{2,1,0:T(8,128)(2,1)S(1)} %fusion.6), channel_id=1, source_target_pairs={{0,18},{2,20},{4,22},{6,24},{8,26},{10,28},{12,30},{16,34},{18,36}... | collective-permute-start | bytes 122888 | tf_op jit(solution)/shard_map/ppermute | solution.py:202
  16.7 9.9 %collective-permute-start.3 = (bf16[2,16,640]{2,1,0:T(8,128)(2,1)S(1)}, bf16[2,16,640]{2,1,0:T(8,128)(2,1)S(1)}, u32[]{:S(2)}, u32[]{:S(2)}) collective-permute-start(bf16[2,16,640]{2,1,0:T(8,128)(2,1)S(1)} %fusion.6), channel_id=1, source_target_pairs={{2,16},{4,18},{6,20},{8,22},{10,24},{12,26},{14,28},{17,3},{18,32}... | collective-permute-start | bytes 122888 | tf_op jit(solution)/shard_map/ppermute | solution.py:202
  23.6 0.9 %copy-start.1 = (bf16[3,3,3,32,32]{4,3,2,1,0:T(8,128)(2,1)S(1)}, bf16[3,3,3,32,32]{4,3,2,1,0:T(8,128)(2,1)}, u32[]{:S(2)}) copy-start(bf16[3,3,3,32,32]{4,3,2,1,0:T(8,128)(2,1)} %param.14) | copy-start | bytes 165892
  24.9 0.7 %copy-start.5 = (f32[32]{0:T(128)S(1)}, f32[32]{0:T(128)}, u32[]{:S(2)}) copy-start(f32[32]{0:T(128)} %param.13) | copy-start | bytes 388
  25.6 0.7 %copy-start.6 = (f32[32]{0:T(128)S(1)}, f32[32]{0:T(128)}, u32[]{:S(2)}) copy-start(f32[32]{0:T(128)} %param.15) | copy-start | bytes 388

commit v2 on v1

--- a/solution.py
+++ b/solution.py
@@ -23,7 +23,7 @@
 
 
 def compute_kernel(
-    own_ref, halo_ref, w1_ref, w2_ref, b1_ref, b2_ref, out_ref,
+    own_ref, far_ref, near_ref, w1_ref, w2_ref, b1_ref, b2_ref, out_ref,
     src_ref, rf_ref, tm_ref, tp_ref, e0_ref, dm_ref, dp_ref, vf_ref, v_ref, h_ref,
     *, planes, columns, depth_count, row_count,
 ):
@@ -39,37 +39,26 @@
     col = lane % columns
     row_bit = (lane // columns) % 2
 
-    for i in range(2):
-        src_ref[i] = halo_ref[0, 128 * i : 128 * i + 128, :]
-        src_ref[2 + i] = own_ref[i, 0:128, :]
-        src_ref[4 + i] = halo_ref[1, 128 * i : 128 * i + 128, :]
+    src_ref[0] = far_ref[0:128]
+    src_ref[1] = near_ref[0]
+    src_ref[2] = own_ref[0, 0:128]
+    src_ref[3] = own_ref[1, 0:128]
+    src_ref[4] = near_ref[1]
+    src_ref[5] = far_ref[128:256]
     half = lax.broadcasted_iota(jnp.int32, (8, 128), 1) < 64
-
-    def put_weights(r, row, w, o):
-        turned = pltpu.roll(o, 64, 1)
-        b0 = jnp.where(half, o, turned)
-        b1 = jnp.where(half, turned, o)
-        below = jnp.concatenate([b0, b0, o, b1, b1], axis=1) < -0.5
-        tm_ref[r, row : row + 8, :] = jnp.where(below, w, 0.0)
-        tp_ref[r, row : row + 8, :] = jnp.where(below, 0.0, 1.0 - w)
-
     for r in range(4):
-        if r == 0:
-            rest = halo_ref[0, 256:320, :]
-        elif r == 3:
-            rest = halo_ref[1, 256:320, :]
-        else:
-            rest = own_ref[r - 1, 128:192, :]
+        rest = far_ref[256:336] if r in (0, 3) else own_ref[r - 1, 128:208]
         rest = rest.astype(F32)
         rf_ref[r] = rest[0:32]
-        for i in range(planes * views // 8):
-            put_weights(r, 8 + 8 * i, rest[32 + 8 * i : 40 + 8 * i], rest[56:64, 128 * i : 128 * i + 128])
-        low_row = (352, 320, 336, 368)[r]
-        high_row = (368, 320, 336, 352)[r]
-        low = halo_ref[0, low_row : low_row + 16, :].astype(F32)
-        high = halo_ref[1, high_row : high_row + 16, :].astype(F32)
-        put_weights(r, 0, low[0:8], low[8:16, 0:128])
-        put_weights(r, 8 + planes * views, high[0:8], high[8:16, 0:128])
+        for i in range((planes + 4) * views // 8):
+            w = rest[32 + 8 * i : 40 + 8 * i]
+            o = rest[72:80, 128 * i : 128 * i + 128]
+            turned = pltpu.roll(o, 64, 1)
+            b0 = jnp.where(half, o, turned)
+            b1 = jnp.where(half, turned, o)
+            below = jnp.concatenate([b0, b0, o, b1, b1], axis=1) < -0.5
+            tm_ref[r, 8 * i : 8 * i + 8, :] = jnp.where(below, w, 0.0)
+            tp_ref[r, 8 * i : 8 * i + 8, :] = jnp.where(below, 0.0, 1.0 - w)
 
     for k in range(3):
         base = rf_ref[core + k]
@@ -175,52 +164,46 @@
     lanes = b * m * columns
     core = lax.axis_index("rows") % 2
 
+    def send(x, step_depth, step_chip, sign_of_core):
+        routes = []
+        for d in range(depth_count):
+            for r in range(row_count):
+                sign = sign_of_core[r % 2]
+                to_d, to_r = d + sign * step_depth, r + 2 * sign * step_chip
+                if 0 <= to_d < depth_count and 0 <= to_r < row_count:
+                    routes.append((d * row_count + r, to_d * row_count + to_r))
+        return lax.ppermute(x, ("depth", "rows"), routes)
+
+    rows = planes * v
     offset = (block_index[:, :, :, 0] - lax.axis_index("rows")).astype(BF16)
-    offset = offset.transpose(2, 1, 0).reshape(planes * v // 8, 8, b, 1)
-    offset = jnp.broadcast_to(offset, (planes * v // 8, 8, b, 64)).transpose(1, 0, 2, 3).reshape(8, -1)
-    offset = jnp.pad(offset, ((0, 0), (0, lanes - offset.shape[1])))
+    offset = offset.transpose(2, 1, 0).reshape(rows // 8, 8, b, 1)
+    offset = jnp.broadcast_to(offset, (rows // 8, 8, b, 64)).transpose(1, 0, 2, 3).reshape(8, -1)
+    weight = pack_blend(blend)
+
+    def edge(i):
+        return jnp.concatenate(
+            [weight[8 * i : 8 * i + 8], jnp.pad(offset[:, 128 * i : 128 * i + 128], ((0, 0), (0, lanes - 128)))], axis=0
+        )
+
+    low = send(edge(rows // 8 - 1), 1, 0, (1, 1))
+    high = send(edge(0), 1, 0, (-1, -1))
     own = jnp.concatenate(
         [
             pack_features(src_feat, groups, per_group, columns),
             pack_features(ref_feat[:, None], groups, per_group, columns),
-            pack_blend(blend),
-            offset,
+            low[0:8],
+            weight,
+            high[0:8],
+            jnp.concatenate([low[8:16, 0:128], offset, high[8:16, 0:128]], axis=1),
         ],
         axis=0,
     )
     pairs = [[2 * i, 2 * i + 1] for i in range(row_count // 2)]
     gathered = lax.all_gather(own, "rows", axis_index_groups=pairs)
-
-    def send(x, step_depth, step_chip):
-        routes = []
-        for d in range(depth_count):
-            for r in range(row_count):
-                sign = 1 if r % 2 == 0 else -1
-                to_d, to_r = d + sign * step_depth, r + 2 * sign * step_chip
-                if 0 <= to_d < depth_count and 0 <= to_r < row_count:
-                    routes.append((d * row_count + r, to_d * row_count + to_r))
-        return lax.ppermute(x, ("depth", "rows"), routes)
-
-    edge_offset = jnp.where(core == 0, gathered[:, 184:192, 256:384], gathered[:, 184:192, 0:128])
-    edge_blend = jnp.where(core == 0, gathered[:, 176:184], gathered[:, 160:168])
-    edge = jnp.concatenate([edge_blend, jnp.pad(edge_offset, ((0, 0), (0, 0), (0, lanes - 128)))], axis=1)
-    from_chip = send(gathered, 0, 1)
-    from_depth = send(edge, 1, 0)
-    from_same = send(edge, 1, 1)
-    from_cross = send(edge, 1, -1)
-    halo = jnp.concatenate(
-        [
-            from_chip[0, 0:128],
-            from_chip[1, 0:128],
-            lax.dynamic_index_in_dim(from_chip, 1 - core, 0, keepdims=False)[128:192],
-            from_depth[0],
-            from_depth[1],
-            lax.dynamic_index_in_dim(from_same, 1 - core, 0, keepdims=False),
-            lax.dynamic_index_in_dim(from_cross, core, 0, keepdims=False),
-        ],
-        axis=0,
-    )
-    halos = lax.all_gather(halo, "rows", axis_index_groups=pairs)
+    rest = lax.dynamic_index_in_dim(gathered, 1 - core, 0, keepdims=False)[128:208]
+    far = send(jnp.concatenate([gathered[0, 0:128], gathered[1, 0:128], rest], axis=0), 0, 1, (1, -1))
+    near = lax.dynamic_slice_in_dim(far, 128 * (1 - core), 128, 0)
+    near = lax.all_gather(near, "rows", axis_index_groups=pairs)
 
     corr = conv_first[..., :groups] * jnp.asarray(0.0625, BF16)
     spread = conv_first[..., groups:].reshape(3, 3, 3, outputs, groups, per_group)
@@ -235,7 +218,7 @@
     out = pl.pallas_call(
         kernel,
         out_shape=jax.ShapeDtypeStruct((planes, outputs, lanes), BF16),
-        in_specs=[pl.BlockSpec(memory_space=pltpu.VMEM)] * 6,
+        in_specs=[pl.BlockSpec(memory_space=pltpu.VMEM)] * 7,
         out_specs=pl.BlockSpec(memory_space=pltpu.VMEM),
         scratch_shapes=[
             pltpu.VMEM((6, 128, lanes), BF16),
@@ -251,7 +234,7 @@
         ],
         compiler_params=pltpu.CompilerParams(vmem_limit_bytes=48 * 1024 * 1024),
         name="volume_and_convolutions",
-    )(gathered, halos, w1, w2, bias_first[:, None], bias_second[:, None])
+    )(gathered, far, near, w1, w2, bias_first[:, None], bias_second[:, None])
     out = out.reshape(planes, outputs, b, m, columns).transpose(2, 0, 3, 1, 4)
     return out.reshape(b, planes, m, outputs * columns)
 

time: 45 us -> 40.7 us (0.904)
  the two profiles are of different devices: /device:TPU:199 before, /device:TPU:287 now
where the time goes in v2:
time: 40.7 us; the launch traced here: 40.5 us
  Pallas kernels  9.59 us (24%)
  starting transfers between devices  8.38 us (21%)
  blocking collectives  8.02 us (20%)
  local copies, waits for them, and re-layouts  7.8 us (19%)
  waiting for transfers between devices  6.15 us (15%)
    pallas_call x1, Pallas kernels, body(): pl.pallas_call(kernel, out_shape=jax.ShapeDtypeStruct((planes, outputs, l...  9.59 us
    ppermute x3, starting transfers between devices, send(): return lax.ppermute(x, ('depth', 'rows'), routes)  8.38 us
    ppermute x3, waiting for transfers between devices, send(): return lax.ppermute(x, ('depth', 'rows'), routes)  6.15 us
    all_gather x1, blocking collectives, body(): near = lax.all_gather(near, 'rows', axis_index_groups=pairs)  4.11 us
    all_gather x1, blocking collectives, body(): gathered = lax.all_gather(own, 'rows', axis_index_groups=pairs)  3.91 us
    unnamed x24, local copies, waits for them, and re-layouts  2.98 us
    reshape x1, local copies, waits for them, and re-layouts, body(): return out.reshape(b, planes, m, outputs * columns)  1.31 us
  transfers between devices with their start and end apart: 3, of which 2 were waited for; matrix products, arithmetic and copies ran while one was open for 7% of the time, Pallas kernels for 0%

profile of v2, /device:TPU:287, one launch (start us, length us, event | category | flops | bytes accessed | tf_op | source)
XLA Modules:
  0.0 40.5 jit_solution(6884079310343182032)
XLA Ops:
  0.0 0.0 copy-start.5
  0.0 0.0 copy-start.3
  0.0 0.7 %copy-done.5 = s32[2,4,6,1]{2,3,1,0:T(1,128)S(1)} copy-done((s32[2,4,6,1]{2,3,1,0:T(1,128)S(1)}, s32[2,4,6,1]{2,3,1,0:T(1,128)}, u32[]{:S(2)}) %copy-start.5) | copy-done | bytes 216
  0.7 0.1 copy.22
  0.8 0.1 broadcast_in_dim.16
  0.9 0.1 copy.23
  1.0 0.1 broadcast_bitcast_fusion
  1.1 0.1 reshape.44
  1.2 0.0 copy-done.3
  1.3 0.1 slice.49
  1.4 4.4 %collective-permute-start = (bf16[16,640]{1,0:T(8,128)(2,1)S(1)}, bf16[16,640]{1,0:T(8,128)(2,1)S(1)}, u32[]{:S(2)}, u32[]{:S(2)}) collective-permute-start(bf16[16,640]{1,0:T(8,128)(2,1)S(1)} %fusion.2), channel_id=1, source_target_pairs={{0,16},{1,17},{2,18},{3,19},{4,20},{5,21},{6,22},{7,23},{8,24},{9,... | collective-permute-start | bytes 61448 | tf_op jit(solution)/shard_map/ppermute | solution.py:175
  5.8 0.0 copy-start.4
  5.8 0.1 slice.53
  5.9 0.0 copy-start.2
  5.9 2.1 %collective-permute-start.1 = (bf16[16,640]{1,0:T(8,128)(2,1)S(1)}, bf16[16,640]{1,0:T(8,128)(2,1)S(1)}, u32[]{:S(2)}, u32[]{:S(2)}) collective-permute-start(bf16[16,640]{1,0:T(8,128)(2,1)S(1)} %fusion.3), channel_id=1, source_target_pairs={{16,0},{17,1},{18,2},{19,3},{20,4},{21,5},{22,6},{23,7},{24,8},{25... | collective-permute-start | bytes 61448 | tf_op jit(solution)/shard_map/ppermute | solution.py:175
  8.0 0.0 copy-done.4
  8.0 0.1 reshape_broadcast_in_dim.3
  8.1 0.1 copy.20
  8.2 0.1 reshape.43
  8.3 0.0 copy-done.2
  8.3 0.3 reshape.41
  8.6 0.3 copy.19
  8.9 0.2 reshape.42
  9.1 0.0 copy-start.6
  9.1 0.0 copy-start
  9.2 0.5 %copy-done.6 = f32[32]{0:T(128)S(1)} copy-done((f32[32]{0:T(128)S(1)}, f32[32]{0:T(128)}, u32[]{:S(2)}) %copy-start.6) | copy-done | bytes 152
  9.7 0.1 copy.31.b1_ref
  9.8 0.0 copy-start.7
  9.8 0.7 %copy-done.7 = f32[32]{0:T(128)S(1)} copy-done((f32[32]{0:T(128)S(1)}, f32[32]{0:T(128)}, u32[]{:S(2)}) %copy-start.7) | copy-done | bytes 152
  10.5 0.1 copy.32.b2_ref
  10.6 0.1 reshape.45
  10.7 0.0 copy-done
  10.7 0.1 slice.62
  10.8 0.1 copy.36
  10.9 0.2 copy.35
  11.2 0.1 pad.11.clone
  11.2 0.0 collective-permute-done
  11.3 0.5 %collective-permute-done.1 = bf16[16,640]{1,0:T(8,128)(2,1)S(1)} collective-permute-done((bf16[16,640]{1,0:T(8,128)(2,1)S(1)}, bf16[16,640]{1,0:T(8,128)(2,1)S(1)}, u32[]{:S(2)}, u32[]{:S(2)}) %collective-permute-start.1) | collective-permute-done | bytes 20512 | tf_op jit(solution)/shard_map/ppermute | solution.py:175
  11.8 3.9 %all-gather = bf16[416,640]{1,0:T(8,128)(2,1)S(1)} all-gather(bf16[208,640]{1,0:T(8,128)(2,1)S(1)} %constant_dynamic-update-slice_fusion), channel_id=2, replica_groups={{0,1},{2,3},{4,5},{6,7},{8,9},{10,11},{12,13},{14,15},{16,17},{18,19},{..., dimensions={0}, use_global_device_ids=true | all-gather | bytes 798720 | tf_op jit(solution)/shard_map/all_gather | solution.py:202
  15.8 1.9 %collective-permute-start.2 = (bf16[336,640]{1,0:T(8,128)(2,1)S(1)}, bf16[336,640]{1,0:T(8,128)(2,1)S(1)}, u32[]{:S(2)}, u32[]{:S(2)}) collective-permute-start(bf16[336,640]{1,0:T(8,128)(2,1)S(1)} %pad_maximum_fusion), channel_id=1, source_target_pairs={{0,2},{2,4},{3,1},{4,6},{5,3},{6,8},{7,5},{8,10},{9,7},{10,12},{11... | collective-permute-start | bytes 1290248 | tf_op jit(solution)/shard_map/ppermute | solution.py:175
  17.8 0.1 maximum_bitcast_fusion
  17.9 0.2 copy.29
  18.2 0.0 copy-start.1
  18.2 0.2 reshape.48.w1_ref
  18.4 0.7 %copy-done.1 = bf16[3,3,3,32,32]{4,3,2,1,0:T(8,128)(2,1)S(1)} copy-done((bf16[3,3,3,32,32]{4,3,2,1,0:T(8,128)(2,1)S(1)}, bf16[3,3,3,32,32]{4,3,2,1,0:T(8,128)(2,1)}, u32[]{:S(2)}) %copy-start.1) | copy-done | bytes 55320
  19.1 0.2 copy.30
  19.3 0.2 reshape.49.w2_ref
  19.4 5.6 %collective-permute-done.2.far_ref = bf16[336,640]{1,0:T(8,128)(2,1)S(1)} collective-permute-done((bf16[336,640]{1,0:T(8,128)(2,1)S(1)}, bf16[336,640]{1,0:T(8,128)(2,1)S(1)}, u32[]{:S(2)}, u32[]{:S(2)}) %collective-permute-start.2) | collective-permute-done | bytes 430112 | tf_op jit(solution)/shard_map/ppermute | solution.py:175
  25.1 4.1 %all-gather.1 = bf16[256,640]{1,0:T(8,128)(2,1)S(1)} all-gather(bf16[128,640]{1,0:T(8,128)(2,1)S(1)} %constant_dynamic-slice_fusion), channel_id=3, replica_groups={{0,1},{2,3},{4,5},{6,7},{8,9},{10,11},{12,13},{14,15},{16,17},{18,19},{..., dimensions={0}, use_global_device_ids=true | all-gather | bytes 491520 | tf_op jit(solution)/shard_map/all_gather | solution.py:206
  29.2 9.6 %volume_and_convolutions.1 = bf16[6,32,640]{2,1,0:T(8,128)(2,1)S(1)} custom-call(bf16[2,208,640]{2,1,0:T(8,128)(2,1)S(1)} %bitcast.37, bf16[336,640]{1,0:T(8,128)(2,1)S(1)} %collective-permute-done.2.far_ref, bf16[2,128,640]{2,1,0:T(8,128)(2,1)S(1)} %bitcast.38, bf16[96,432]{1,0:T(8,128)(2,1)S(1)} %reshape.48.w1_ref, bf16[96,288]{1,0:T(8,128)(2,1)S(1)} %reshape.49.w2_ref, ...), custom_call_target="tpu_custom_call" | custom-call | tf_op jit(solution)/shard_map/volume_and_convolutions/pallas_call | solution.py:218
  38.8 0.3 reshape.50
  39.1 0.1 copy.33
  39.2 1.3 %reshape.51 = bf16[2,6,2,5120]{3,2,1,0:T(2,128)(2,1)} reshape(bf16[2,6,2,32,160]{4,3,2,1,0:T(8,128)(2,1)S(1)} %copy.33) | data formatting | bytes 491520 | tf_op jit(solution)/shard_map/reshape | solution.py:239
  (24 shorter events, 0.3 us)
Async XLA Ops:
  0.0 0.7 %copy-start.5 = (s32[2,4,6,1]{2,3,1,0:T(1,128)S(1)}, s32[2,4,6,1]{2,3,1,0:T(1,128)}, u32[]{:S(2)}) copy-start(s32[2,4,6,1]{2,3,1,0:T(1,128)} %param.10) | copy-start | bytes 580
  0.0 1.2 %copy-start.3 = (bf16[2,4,6,2,160]{4,3,2,1,0:T(2,128)(2,1)S(1)}, bf16[2,4,6,2,160]{4,3,2,1,0:T(2,128)(2,1)}, u32[]{:S(2)}) copy-start(bf16[2,4,6,2,160]{4,3,2,1,0:T(2,128)(2,1)} %param.11) | copy-start | bytes 92164
  1.4 9.9 %collective-permute-start = (bf16[16,640]{1,0:T(8,128)(2,1)S(1)}, bf16[16,640]{1,0:T(8,128)(2,1)S(1)}, u32[]{:S(2)}, u32[]{:S(2)}) collective-permute-start(bf16[16,640]{1,0:T(8,128)(2,1)S(1)} %fusion.2), channel_id=1, source_target_pairs={{0,16},{1,17},{2,18},{3,19},{4,20},{5,21},{6,22},{7,23},{8,24},{9,... | collective-permute-start | bytes 61448 | tf_op jit(solution)/shard_map/ppermute | solution.py:175
  5.8 2.2 %copy-start.4 = (bf16[2,2,5120]{2,1,0:T(2,128)(2,1)S(1)}, bf16[2,2,5120]{2,1,0:T(2,128)(2,1)}, u32[]{:S(2)}) copy-start(bf16[2,2,5120]{2,1,0:T(2,128)(2,1)} %param.8) | copy-start | bytes 122884
  5.9 2.4 %copy-start.2 = (bf16[2,4,2,5120]{3,2,1,0:T(2,128)(2,1)S(1)}, bf16[2,4,2,5120]{3,2,1,0:T(2,128)(2,1)}, u32[]{:S(2)}) copy-start(bf16[2,4,2,5120]{3,2,1,0:T(2,128)(2,1)} %param.9) | copy-start | bytes 491524
  5.9 5.9 %collective-permute-start.1 = (bf16[16,640]{1,0:T(8,128)(2,1)S(1)}, bf16[16,640]{1,0:T(8,128)(2,1)S(1)}, u32[]{:S(2)}, u32[]{:S(2)}) collective-permute-start(bf16[16,640]{1,0:T(8,128)(2,1)S(1)} %fusion.3), channel_id=1, source_target_pairs={{16,0},{17,1},{18,2},{19,3},{20,4},{21,5},{22,6},{23,7},{24,8},{25... | collective-permute-start | bytes 61448 | tf_op jit(solution)/shard_map/ppermute | solution.py:175
  9.1 0.7 %copy-start.6 = (f32[32]{0:T(128)S(1)}, f32[32]{0:T(128)}, u32[]{:S(2)}) copy-start(f32[32]{0:T(128)} %param.13) | copy-start | bytes 388
  9.1 1.6 %copy-start = (bf16[3,3,3,32,40]{4,3,2,1,0:T(8,128)(2,1)S(1)}, bf16[3,3,3,32,40]{4,3,2,1,0:T(8,128)(2,1)}, u32[]{:S(2)}) copy-start(bf16[3,3,3,32,40]{4,3,2,1,0:T(8,128)(2,1)} %param.12) | copy-start | bytes 207364
  9.8 0.7 %copy-start.7 = (f32[32]{0:T(128)S(1)}, f32[32]{0:T(128)}, u32[]{:S(2)}) copy-start(f32[32]{0:T(128)} %param.15) | copy-start | bytes 388
  15.8 9.2 %collective-permute-start.2 = (bf16[336,640]{1,0:T(8,128)(2,1)S(1)}, bf16[336,640]{1,0:T(8,128)(2,1)S(1)}, u32[]{:S(2)}, u32[]{:S(2)}) collective-permute-start(bf16[336,640]{1,0:T(8,128)(2,1)S(1)} %pad_maximum_fusion), channel_id=1, source_target_pairs={{0,2},{2,4},{3,1},{4,6},{5,3},{6,8},{7,5},{8,10},{9,7},{10,12},{11... | collective-permute-start | bytes 1290248 | tf_op jit(solution)/shard_map/ppermute | solution.py:175
  18.2 0.9 %copy-start.1 = (bf16[3,3,3,32,32]{4,3,2,1,0:T(8,128)(2,1)S(1)}, bf16[3,3,3,32,32]{4,3,2,1,0:T(8,128)(2,1)}, u32[]{:S(2)}) copy-start(bf16[3,3,3,32,32]{4,3,2,1,0:T(8,128)(2,1)} %param.14) | copy-start | bytes 165892

commit v3 on v2

--- a/solution.py
+++ b/solution.py
@@ -14,12 +14,12 @@
 def pack_features(rows, groups, per_group, columns):
     b, v, m, _ = rows.shape
     x = rows.reshape(b, v, m, groups, per_group, columns)
-    return x.transpose(1, 4, 3, 0, 2, 5).reshape(v * per_group * groups, b * m * columns)
+    return x.transpose(1, 4, 3, 2, 0, 5).reshape(v * per_group * groups, b * m * columns)
 
 
 def pack_blend(weight):
     b, v, p, m, w = weight.shape
-    return weight.transpose(2, 1, 0, 3, 4).reshape(p * v, b * m * w)
+    return weight.transpose(2, 1, 3, 0, 4).reshape(p * v, b * m * w)
 
 
 def compute_kernel(
@@ -37,7 +37,8 @@
 
     lane = lax.broadcasted_iota(jnp.int32, (1, lanes), 1)
     col = lane % columns
-    row_bit = (lane // columns) % 2
+    second = lane >= lanes // 2
+    scene = (lane // columns) % 2 == 1
 
     src_ref[0] = far_ref[0:128]
     src_ref[1] = near_ref[0]
@@ -56,7 +57,8 @@
             turned = pltpu.roll(o, 64, 1)
             b0 = jnp.where(half, o, turned)
             b1 = jnp.where(half, turned, o)
-            below = jnp.concatenate([b0, b0, o, b1, b1], axis=1) < -0.5
+            tiles = lanes // 128
+            below = jnp.where(scene, jnp.concatenate([b1] * tiles, axis=1), jnp.concatenate([b0] * tiles, axis=1)) < -0.5
             tm_ref[r, 8 * i : 8 * i + 8, :] = jnp.where(below, w, 0.0)
             tp_ref[r, 8 * i : 8 * i + 8, :] = jnp.where(below, 0.0, 1.0 - w)
 
@@ -69,16 +71,23 @@
             dm_ref[k, v] = src_ref[core + k, rows, :].astype(F32) - middle
             dp_ref[k, v] = src_ref[core + k + 2, rows, :].astype(F32) - middle
 
-    def volume_plane(pair, carry):
-        outside = ((pair == 0) & first) | ((pair == planes // 2 + 1) & last)
-        row = pl.multiple_of(pair * 8, 8)
+    def mixed(upper, lower):
+        return pltpu.roll(jnp.where(second, upper, lower), lanes // 2, 1)
+
+    def volume_planes(pair):
+        outside = first if pair == 0 else last if pair == planes // 2 + 1 else False
+        row = 8 * pair
         for k in range(3):
-            missing = outside | ((k == 0) & (q == 0)) | ((k == 2) & (q == row_count - 1))
+            missing = outside
+            if k == 0:
+                missing = missing | (q == 0)
+            if k == 2:
+                missing = missing | (q == row_count - 1)
             keep = jnp.where(missing, 0.0, 1.0).astype(F32)
             for i in range(lanes // 128):
                 cols = slice(128 * i, 128 * i + 128)
-                tm = tm_ref[core + k, pl.ds(row, 8), cols]
-                tp = tp_ref[core + k, pl.ds(row, 8), cols]
+                tm = tm_ref[core + k, row : row + 8, cols]
+                tp = tp_ref[core + k, row : row + 8, cols]
                 base = rf_ref[core + k, :, cols]
                 for t in range(2):
                     total = jnp.zeros((32, 128), F32)
@@ -92,23 +101,17 @@
                     spread = squares * (0.2 * keep) - total * total * (0.04 * keep)
                     product = base * (total + 4.0 * base)
                     corr = (product[0:8] + product[8:16] + product[16:24] + product[24:32]) * keep
-                    vf_ref[t, k, 0:32, cols] = spread
-                    vf_ref[t, k, 32:40, cols] = corr
+                    vf_ref[pair % 2, t, k, 0:32, cols] = spread
+                    vf_ref[pair % 2, t, k, 32:40, cols] = corr
         for t in range(2):
             p = 2 * pair + t
             for k in range(3):
-                v_ref[p, 96 * k : 96 * k + 48, :] = vf_ref[t, k].astype(BF16)
+                v_ref[p, 96 * k : 96 * k + 48, :] = vf_ref[pair % 2, t, k].astype(BF16)
             for k in range(2):
-                mixed = jnp.where(
-                    row_bit == 0,
-                    pltpu.roll(vf_ref[t, k], lanes - columns, 1),
-                    pltpu.roll(vf_ref[t, k + 1], columns, 1),
-                )
-                v_ref[p, 96 * k + 48 : 96 * k + 96, :] = mixed.astype(BF16)
-        return carry
-
-    vf_ref[:, :, 40:48, :] = jnp.zeros((2, 3, 8, lanes), F32)
-    lax.fori_loop(0, planes // 2 + 2, volume_plane, 0)
+                between = mixed(vf_ref[pair % 2, t, k], vf_ref[pair % 2, t, k + 1])
+                v_ref[p, 96 * k + 48 : 96 * k + 96, :] = between.astype(BF16)
+
+    vf_ref[:, :, :, 40:48, :] = jnp.zeros((2, 2, 3, 8, lanes), F32)
 
     def shifted_sum(parts, width):
         column = jnp.concatenate([col] * (width // lanes), axis=1)
@@ -116,39 +119,44 @@
         right = jnp.where(column == columns - 1, 0.0, pltpu.roll(parts[64:96], width - 1, 1))
         return parts[32:64] + left + right
 
-    lost = jnp.concatenate(
+    inside = jnp.concatenate(
         [
-            jnp.where((row_bit == 0) & (q == 0), 0.0, 1.0),
-            jnp.where((row_bit == 1) & (q == row_count - 1), 0.0, 1.0),
+            jnp.where(second | (q != 0), 1.0, 0.0),
+            jnp.where(second & (q == row_count - 1), 0.0, 1.0),
         ],
         axis=1,
     )
 
-    def hidden_plane(p, carry):
+    def hidden_plane(p):
         upper = jnp.concatenate([v_ref[p + a, 0:144, :] for a in range(3)], axis=0)
         lower = jnp.concatenate([v_ref[p + a, 96:240, :] for a in range(3)], axis=0)
         taps = jnp.concatenate([upper, lower], axis=1)
         parts = jnp.dot(w1_ref[...], taps, preferred_element_type=F32)
-        missing = ((p == 0) & first) | ((p == planes + 1) & last)
-        keep = lost * jnp.where(missing, 0.0, 1.0).astype(F32)
+        keep = inside
+        if p == 0:
+            keep = keep * jnp.where(first, 0.0, 1.0).astype(F32)
+        if p == planes + 1:
+            keep = keep * jnp.where(last, 0.0, 1.0).astype(F32)
         hidden = jnp.maximum(shifted_sum(parts, 2 * lanes) + b1_ref[...], 0.0) * keep
         above = hidden[:, :lanes]
         below = hidden[:, lanes:]
         h_ref[p, 0:32, :] = above.astype(BF16)
+        h_ref[p, 32:64, :] = mixed(above, below).astype(BF16)
         h_ref[p, 64:96, :] = below.astype(BF16)
-        mixed = jnp.where(row_bit == 0, pltpu.roll(above, lanes - columns, 1), pltpu.roll(below, columns, 1))
-        h_ref[p, 32:64, :] = mixed.astype(BF16)
-        return carry
-
-    lax.fori_loop(0, planes + 2, hidden_plane, 0)
-
-    def out_plane(p, carry):
+
+    def out_plane(p):
         taps = jnp.concatenate([h_ref[p + a] for a in range(3)], axis=0)
         parts = jnp.dot(w2_ref[...], taps, preferred_element_type=F32)
         out_ref[p] = (shifted_sum(parts, lanes) + b2_ref[...]).astype(BF16)
-        return carry
-
-    lax.fori_loop(0, planes, out_plane, 0)
+
+    for pair in range(planes // 2 + 2):
+        volume_planes(pair)
+        if pair >= 1:
+            hidden_plane(2 * pair - 2)
+            hidden_plane(2 * pair - 1)
+        if pair >= 2:
+            out_plane(2 * pair - 4)
+            out_plane(2 * pair - 3)
 
 
 def body(ref_feat, src_feat, block_index, blend, conv_first, bias_first, conv_second, bias_second):
@@ -228,14 +236,14 @@
             pltpu.VMEM((3, v, 32, lanes), F32),
             pltpu.VMEM((3, v, 32, lanes), F32),
             pltpu.VMEM((3, v, 32, lanes), F32),
-            pltpu.VMEM((2, 3, 48, lanes), F32),
+            pltpu.VMEM((2, 2, 3, 48, lanes), F32),
             pltpu.VMEM((planes + 4, 240, lanes), BF16),
             pltpu.VMEM((planes + 2, 96, lanes), BF16),
         ],
         compiler_params=pltpu.CompilerParams(vmem_limit_bytes=48 * 1024 * 1024),
         name="volume_and_convolutions",
     )(gathered, far, near, w1, w2, bias_first[:, None], bias_second[:, None])
-    out = out.reshape(planes, outputs, b, m, columns).transpose(2, 0, 3, 1, 4)
+    out = out.reshape(planes, outputs, m, b, columns).transpose(3, 0, 2, 1, 4)
     return out.reshape(b, planes, m, outputs * columns)
 
 

time: 40.7 us -> 37 us (0.909)
  the two profiles are of different devices: /device:TPU:287 before, /device:TPU:281 now
where the time goes in v3:
time: 37 us; the launch traced here: 36.7 us
  starting transfers between devices  8.38 us (23%)
  blocking collectives  8.02 us (22%)
  local copies, waits for them, and re-layouts  7.79 us (21%)
  waiting for transfers between devices  6.15 us (17%)
  Pallas kernels  5.87 us (16%)
    ppermute x3, starting transfers between devices, send(): return lax.ppermute(x, ('depth', 'rows'), routes)  8.38 us
    ppermute x3, waiting for transfers between devices, send(): return lax.ppermute(x, ('depth', 'rows'), routes)  6.15 us
    pallas_call x1, Pallas kernels, body(): pl.pallas_call(kernel, out_shape=jax.ShapeDtypeStruct((planes, outputs, l...  5.87 us
    all_gather x1, blocking collectives, body(): near = lax.all_gather(near, 'rows', axis_index_groups=pairs)  4.11 us
    all_gather x1, blocking collectives, body(): gathered = lax.all_gather(own, 'rows', axis_index_groups=pairs)  3.91 us
    unnamed x24, local copies, waits for them, and re-layouts  2.97 us
    reshape x1, local copies, waits for them, and re-layouts, body(): return out.reshape(b, planes, m, outputs * columns)  1.31 us
  transfers between devices with their start and end apart: 3, of which 2 were waited for; matrix products, arithmetic and copies ran while one was open for 8% of the time, Pallas kernels for 0%

profile of v3, /device:TPU:281, one launch (start us, length us, event | category | flops | bytes accessed | tf_op | source)
XLA Modules:
  0.0 36.7 jit_solution(6207216017834917479)
XLA Ops:
  0.0 0.0 copy-start.5
  0.0 0.0 copy-start.3
  0.0 0.7 %copy-done.5 = s32[2,4,6,1]{2,3,1,0:T(1,128)S(1)} copy-done((s32[2,4,6,1]{2,3,1,0:T(1,128)S(1)}, s32[2,4,6,1]{2,3,1,0:T(1,128)}, u32[]{:S(2)}) %copy-start.5) | copy-done | bytes 216
  0.7 0.1 copy.22
  0.8 0.1 broadcast_in_dim.16
  0.9 0.1 copy.23
  1.0 0.1 broadcast_bitcast_fusion
  1.1 0.1 reshape.44
  1.2 0.0 copy-done.3
  1.3 0.1 slice.49
  1.4 4.4 %collective-permute-start = (bf16[16,640]{1,0:T(8,128)(2,1)S(1)}, bf16[16,640]{1,0:T(8,128)(2,1)S(1)}, u32[]{:S(2)}, u32[]{:S(2)}) collective-permute-start(bf16[16,640]{1,0:T(8,128)(2,1)S(1)} %fusion.2), channel_id=1, source_target_pairs={{0,16},{1,17},{2,18},{3,19},{4,20},{5,21},{6,22},{7,23},{8,24},{9,... | collective-permute-start | bytes 61448 | tf_op jit(solution)/shard_map/ppermute | solution.py:183
  5.8 0.0 copy-start.4
  5.8 0.1 slice.53
  5.9 0.0 copy-start.2
  5.9 2.1 %collective-permute-start.1 = (bf16[16,640]{1,0:T(8,128)(2,1)S(1)}, bf16[16,640]{1,0:T(8,128)(2,1)S(1)}, u32[]{:S(2)}, u32[]{:S(2)}) collective-permute-start(bf16[16,640]{1,0:T(8,128)(2,1)S(1)} %fusion.3), channel_id=1, source_target_pairs={{16,0},{17,1},{18,2},{19,3},{20,4},{21,5},{22,6},{23,7},{24,8},{25... | collective-permute-start | bytes 61448 | tf_op jit(solution)/shard_map/ppermute | solution.py:183
  8.0 0.0 copy-done.4
  8.0 0.1 reshape_broadcast_in_dim.3
  8.1 0.1 copy.20
  8.2 0.1 reshape.43
  8.3 0.0 copy-done.2
  8.3 0.3 reshape.41
  8.6 0.3 copy.19
  8.9 0.2 reshape.42
  9.1 0.0 copy-start.6
  9.1 0.0 copy-start
  9.2 0.5 %copy-done.6 = f32[32]{0:T(128)S(1)} copy-done((f32[32]{0:T(128)S(1)}, f32[32]{0:T(128)}, u32[]{:S(2)}) %copy-start.6) | copy-done | bytes 152
  9.7 0.1 copy.31.b1_ref
  9.8 0.0 copy-start.7
  9.8 0.7 %copy-done.7 = f32[32]{0:T(128)S(1)} copy-done((f32[32]{0:T(128)S(1)}, f32[32]{0:T(128)}, u32[]{:S(2)}) %copy-start.7) | copy-done | bytes 152
  10.5 0.1 copy.32.b2_ref
  10.6 0.1 reshape.45
  10.7 0.0 copy-done
  10.7 0.1 slice.62
  10.8 0.1 copy.36
  10.9 0.2 copy.35
  11.2 0.1 pad.11.clone
  11.2 0.0 collective-permute-done
  11.3 0.5 %collective-permute-done.1 = bf16[16,640]{1,0:T(8,128)(2,1)S(1)} collective-permute-done((bf16[16,640]{1,0:T(8,128)(2,1)S(1)}, bf16[16,640]{1,0:T(8,128)(2,1)S(1)}, u32[]{:S(2)}, u32[]{:S(2)}) %collective-permute-start.1) | collective-permute-done | bytes 20512 | tf_op jit(solution)/shard_map/ppermute | solution.py:183
  11.8 3.9 %all-gather = bf16[416,640]{1,0:T(8,128)(2,1)S(1)} all-gather(bf16[208,640]{1,0:T(8,128)(2,1)S(1)} %constant_dynamic-update-slice_fusion), channel_id=2, replica_groups={{0,1},{2,3},{4,5},{6,7},{8,9},{10,11},{12,13},{14,15},{16,17},{18,19},{..., dimensions={0}, use_global_device_ids=true | all-gather | bytes 798720 | tf_op jit(solution)/shard_map/all_gather | solution.py:210
  15.8 1.9 %collective-permute-start.2 = (bf16[336,640]{1,0:T(8,128)(2,1)S(1)}, bf16[336,640]{1,0:T(8,128)(2,1)S(1)}, u32[]{:S(2)}, u32[]{:S(2)}) collective-permute-start(bf16[336,640]{1,0:T(8,128)(2,1)S(1)} %pad_maximum_fusion), channel_id=1, source_target_pairs={{0,2},{2,4},{3,1},{4,6},{5,3},{6,8},{7,5},{8,10},{9,7},{10,12},{11... | collective-permute-start | bytes 1290248 | tf_op jit(solution)/shard_map/ppermute | solution.py:183
  17.8 0.1 maximum_bitcast_fusion
  17.9 0.2 copy.29
  18.2 0.0 copy-start.1
  18.2 0.2 reshape.48.w1_ref
  18.4 0.7 %copy-done.1 = bf16[3,3,3,32,32]{4,3,2,1,0:T(8,128)(2,1)S(1)} copy-done((bf16[3,3,3,32,32]{4,3,2,1,0:T(8,128)(2,1)S(1)}, bf16[3,3,3,32,32]{4,3,2,1,0:T(8,128)(2,1)}, u32[]{:S(2)}) %copy-start.1) | copy-done | bytes 55320
  19.1 0.2 copy.30
  19.3 0.2 reshape.49.w2_ref
  19.4 5.6 %collective-permute-done.2.far_ref = bf16[336,640]{1,0:T(8,128)(2,1)S(1)} collective-permute-done((bf16[336,640]{1,0:T(8,128)(2,1)S(1)}, bf16[336,640]{1,0:T(8,128)(2,1)S(1)}, u32[]{:S(2)}, u32[]{:S(2)}) %collective-permute-start.2) | collective-permute-done | bytes 430112 | tf_op jit(solution)/shard_map/ppermute | solution.py:183
  25.1 4.1 %all-gather.1 = bf16[256,640]{1,0:T(8,128)(2,1)S(1)} all-gather(bf16[128,640]{1,0:T(8,128)(2,1)S(1)} %constant_dynamic-slice_fusion), channel_id=3, replica_groups={{0,1},{2,3},{4,5},{6,7},{8,9},{10,11},{12,13},{14,15},{16,17},{18,19},{..., dimensions={0}, use_global_device_ids=true | all-gather | bytes 491520 | tf_op jit(solution)/shard_map/all_gather | solution.py:214
  29.2 5.9 %volume_and_convolutions.1 = bf16[6,32,640]{2,1,0:T(8,128)(2,1)S(1)} custom-call(bf16[2,208,640]{2,1,0:T(8,128)(2,1)S(1)} %bitcast.37, bf16[336,640]{1,0:T(8,128)(2,1)S(1)} %collective-permute-done.2.far_ref, bf16[2,128,640]{2,1,0:T(8,128)(2,1)S(1)} %bitcast.38, bf16[96,432]{1,0:T(8,128)(2,1)S(1)} %reshape.48.w1_ref, bf16[96,288]{1,0:T(8,128)(2,1)S(1)} %reshape.49.w2_ref, ...), custom_call_target="tpu_custom_call" | custom-call | tf_op jit(solution)/shard_map/volume_and_convolutions/pallas_call | solution.py:226
  35.1 0.3 reshape.50
  35.4 0.1 copy.33
  35.4 1.3 %reshape.51 = bf16[2,6,2,5120]{3,2,1,0:T(2,128)(2,1)} reshape(bf16[2,6,2,32,160]{4,3,2,1,0:T(8,128)(2,1)S(1)} %copy.33) | data formatting | bytes 491520 | tf_op jit(solution)/shard_map/reshape | solution.py:247
  (24 shorter events, 0.3 us)
Async XLA Ops:
  0.0 0.7 %copy-start.5 = (s32[2,4,6,1]{2,3,1,0:T(1,128)S(1)}, s32[2,4,6,1]{2,3,1,0:T(1,128)}, u32[]{:S(2)}) copy-start(s32[2,4,6,1]{2,3,1,0:T(1,128)} %param.10) | copy-start | bytes 580
  0.0 1.2 %copy-start.3 = (bf16[2,4,6,2,160]{4,3,2,1,0:T(2,128)(2,1)S(1)}, bf16[2,4,6,2,160]{4,3,2,1,0:T(2,128)(2,1)}, u32[]{:S(2)}) copy-start(bf16[2,4,6,2,160]{4,3,2,1,0:T(2,128)(2,1)} %param.11) | copy-start | bytes 92164
  1.4 9.9 %collective-permute-start = (bf16[16,640]{1,0:T(8,128)(2,1)S(1)}, bf16[16,640]{1,0:T(8,128)(2,1)S(1)}, u32[]{:S(2)}, u32[]{:S(2)}) collective-permute-start(bf16[16,640]{1,0:T(8,128)(2,1)S(1)} %fusion.2), channel_id=1, source_target_pairs={{0,16},{1,17},{2,18},{3,19},{4,20},{5,21},{6,22},{7,23},{8,24},{9,... | collective-permute-start | bytes 61448 | tf_op jit(solution)/shard_map/ppermute | solution.py:183
  5.8 2.2 %copy-start.4 = (bf16[2,2,5120]{2,1,0:T(2,128)(2,1)S(1)}, bf16[2,2,5120]{2,1,0:T(2,128)(2,1)}, u32[]{:S(2)}) copy-start(bf16[2,2,5120]{2,1,0:T(2,128)(2,1)} %param.8) | copy-start | bytes 122884
  5.9 2.4 %copy-start.2 = (bf16[2,4,2,5120]{3,2,1,0:T(2,128)(2,1)S(1)}, bf16[2,4,2,5120]{3,2,1,0:T(2,128)(2,1)}, u32[]{:S(2)}) copy-start(bf16[2,4,2,5120]{3,2,1,0:T(2,128)(2,1)} %param.9) | copy-start | bytes 491524
  5.9 5.9 %collective-permute-start.1 = (bf16[16,640]{1,0:T(8,128)(2,1)S(1)}, bf16[16,640]{1,0:T(8,128)(2,1)S(1)}, u32[]{:S(2)}, u32[]{:S(2)}) collective-permute-start(bf16[16,640]{1,0:T(8,128)(2,1)S(1)} %fusion.3), channel_id=1, source_target_pairs={{16,0},{17,1},{18,2},{19,3},{20,4},{21,5},{22,6},{23,7},{24,8},{25... | collective-permute-start | bytes 61448 | tf_op jit(solution)/shard_map/ppermute | solution.py:183
  9.1 0.7 %copy-start.6 = (f32[32]{0:T(128)S(1)}, f32[32]{0:T(128)}, u32[]{:S(2)}) copy-start(f32[32]{0:T(128)} %param.13) | copy-start | bytes 388
  9.1 1.6 %copy-start = (bf16[3,3,3,32,40]{4,3,2,1,0:T(8,128)(2,1)S(1)}, bf16[3,3,3,32,40]{4,3,2,1,0:T(8,128)(2,1)}, u32[]{:S(2)}) copy-start(bf16[3,3,3,32,40]{4,3,2,1,0:T(8,128)(2,1)} %param.12) | copy-start | bytes 207364
  9.8 0.7 %copy-start.7 = (f32[32]{0:T(128)S(1)}, f32[32]{0:T(128)}, u32[]{:S(2)}) copy-start(f32[32]{0:T(128)} %param.15) | copy-start | bytes 388
  15.8 9.2 %collective-permute-start.2 = (bf16[336,640]{1,0:T(8,128)(2,1)S(1)}, bf16[336,640]{1,0:T(8,128)(2,1)S(1)}, u32[]{:S(2)}, u32[]{:S(2)}) collective-permute-start(bf16[336,640]{1,0:T(8,128)(2,1)S(1)} %pad_maximum_fusion), channel_id=1, source_target_pairs={{0,2},{2,4},{3,1},{4,6},{5,3},{6,8},{7,5},{8,10},{9,7},{10,12},{11... | collective-permute-start | bytes 1290248 | tf_op jit(solution)/shard_map/ppermute | solution.py:183
  18.2 0.9 %copy-start.1 = (bf16[3,3,3,32,32]{4,3,2,1,0:T(8,128)(2,1)S(1)}, bf16[3,3,3,32,32]{4,3,2,1,0:T(8,128)(2,1)}, u32[]{:S(2)}) copy-start(bf16[3,3,3,32,32]{4,3,2,1,0:T(8,128)(2,1)} %param.14) | copy-start | bytes 165892

commit v4 on v3

--- a/solution.py
+++ b/solution.py
@@ -23,8 +23,8 @@
 
 
 def compute_kernel(
-    own_ref, far_ref, near_ref, w1_ref, w2_ref, b1_ref, b2_ref, out_ref,
-    src_ref, rf_ref, tm_ref, tp_ref, e0_ref, dm_ref, dp_ref, vf_ref, v_ref, h_ref,
+    own_ref, rest_ref, far_ref, near_ref, w1_ref, w2_ref, b1_ref, b2_ref, out_ref,
+    src_ref, rf_ref, tm_ref, tp_ref, e0_ref, dm_ref, dp_ref, vf_ref, v_ref, h_ref, o_ref,
     *, planes, columns, depth_count, row_count,
 ):
     q = lax.axis_index("rows")
@@ -48,7 +48,7 @@
     src_ref[5] = far_ref[128:256]
     half = lax.broadcasted_iota(jnp.int32, (8, 128), 1) < 64
     for r in range(4):
-        rest = far_ref[256:336] if r in (0, 3) else own_ref[r - 1, 128:208]
+        rest = far_ref[256:336] if r in (0, 3) else rest_ref[r - 1]
         rest = rest.astype(F32)
         rf_ref[r] = rest[0:32]
         for i in range((planes + 4) * views // 8):
@@ -127,6 +127,10 @@
         axis=1,
     )
 
+    diagonal = lax.broadcasted_iota(jnp.int32, (32, 32), 0) == lax.broadcasted_iota(jnp.int32, (32, 32), 1)
+    bias_first = jnp.sum(jnp.where(diagonal, b1_ref[...], 0.0), axis=1, keepdims=True)
+    bias_second = jnp.sum(jnp.where(diagonal, b2_ref[...], 0.0), axis=1, keepdims=True)
+
     def hidden_plane(p):
         upper = jnp.concatenate([v_ref[p + a, 0:144, :] for a in range(3)], axis=0)
         lower = jnp.concatenate([v_ref[p + a, 96:240, :] for a in range(3)], axis=0)
@@ -137,7 +141,7 @@
             keep = keep * jnp.where(first, 0.0, 1.0).astype(F32)
         if p == planes + 1:
             keep = keep * jnp.where(last, 0.0, 1.0).astype(F32)
-        hidden = jnp.maximum(shifted_sum(parts, 2 * lanes) + b1_ref[...], 0.0) * keep
+        hidden = jnp.maximum(shifted_sum(parts, 2 * lanes) + bias_first, 0.0) * keep
         above = hidden[:, :lanes]
         below = hidden[:, lanes:]
         h_ref[p, 0:32, :] = above.astype(BF16)
@@ -147,7 +151,13 @@
     def out_plane(p):
         taps = jnp.concatenate([h_ref[p + a] for a in range(3)], axis=0)
         parts = jnp.dot(w2_ref[...], taps, preferred_element_type=F32)
-        out_ref[p] = (shifted_sum(parts, lanes) + b2_ref[...]).astype(BF16)
+        result = shifted_sum(parts, lanes) + bias_second
+        for m in range(2):
+            for b in range(2):
+                at = 32 * ((b * planes + p) * 2 + m)
+                start = (2 * m + b) * columns
+                o_ref[0, at : at + 32, :] = result[:, start : start + 128]
+                o_ref[1, at : at + 32, 0 : columns - 128] = result[:, start + 128 : start + columns]
 
     for pair in range(planes // 2 + 2):
         volume_planes(pair)
@@ -157,6 +167,14 @@
         if pair >= 2:
             out_plane(2 * pair - 4)
             out_plane(2 * pair - 3)
+
+    for g in range(4 * planes // 8):
+        for a in range(8):
+            pieces = []
+            for j in range(4):
+                rows = pl.ds(256 * g + 4 * a + j, 8, stride=32)
+                pieces += [o_ref[0, rows, :], o_ref[1, rows, :][:, : columns - 128]]
+            out_ref[8 * g : 8 * g + 8, 4 * columns * a : 4 * columns * (a + 1)] = jnp.concatenate(pieces, axis=1).astype(BF16)
 
 
 def body(ref_feat, src_feat, block_index, blend, conv_first, bias_first, conv_second, bias_second):
@@ -186,29 +204,27 @@
     offset = (block_index[:, :, :, 0] - lax.axis_index("rows")).astype(BF16)
     offset = offset.transpose(2, 1, 0).reshape(rows // 8, 8, b, 1)
     offset = jnp.broadcast_to(offset, (rows // 8, 8, b, 64)).transpose(1, 0, 2, 3).reshape(8, -1)
-    weight = pack_blend(blend)
-
-    def edge(i):
-        return jnp.concatenate(
-            [weight[8 * i : 8 * i + 8], jnp.pad(offset[:, 128 * i : 128 * i + 128], ((0, 0), (0, lanes - 128)))], axis=0
-        )
-
-    low = send(edge(rows // 8 - 1), 1, 0, (1, 1))
-    high = send(edge(0), 1, 0, (-1, -1))
+    small = jnp.concatenate([pack_blend(blend), jnp.pad(offset, ((0, 0), (0, lanes - offset.shape[1])))], axis=0)
+    pairs = [[2 * i, 2 * i + 1] for i in range(row_count // 2)]
+    weights = lax.all_gather(small, "rows", axis_index_groups=pairs)
+    edge_blend = jnp.where(core == 0, weights[:, rows - 8 : rows], weights[:, 0:8])
+    edge_offset = jnp.where(core == 0, weights[:, rows:, 16 * rows - 128 : 16 * rows], weights[:, rows:, 0:128])
+    edge_offset = jnp.pad(edge_offset, ((0, 0), (0, 0), (0, lanes - 128)))
+    edges = send(jnp.concatenate([edge_blend, edge_offset], axis=1), 1, 0, (1, -1))
     own = jnp.concatenate(
         [
             pack_features(src_feat, groups, per_group, columns),
             pack_features(ref_feat[:, None], groups, per_group, columns),
-            low[0:8],
-            weight,
-            high[0:8],
-            jnp.concatenate([low[8:16, 0:128], offset, high[8:16, 0:128]], axis=1),
+            edges.reshape(32, lanes),
         ],
         axis=0,
     )
-    pairs = [[2 * i, 2 * i + 1] for i in range(row_count // 2)]
     gathered = lax.all_gather(own, "rows", axis_index_groups=pairs)
-    rest = lax.dynamic_index_in_dim(gathered, 1 - core, 0, keepdims=False)[128:208]
+    low = gathered[0, 160:192].reshape(2, 16, lanes)
+    high = gathered[1, 160:192].reshape(2, 16, lanes)
+    offsets = jnp.concatenate([low[:, 8:, :128], weights[:, rows:, : 16 * rows], high[:, 8:, :128]], axis=2)
+    rests = jnp.concatenate([gathered[:, 128:160], low[:, 0:8], weights[:, :rows], high[:, 0:8], offsets], axis=1)
+    rest = lax.dynamic_index_in_dim(rests, 1 - core, 0, keepdims=False)
     far = send(jnp.concatenate([gathered[0, 0:128], gathered[1, 0:128], rest], axis=0), 0, 1, (1, -1))
     near = lax.dynamic_slice_in_dim(far, 128 * (1 - core), 128, 0)
     near = lax.all_gather(near, "rows", axis_index_groups=pairs)
@@ -225,8 +241,8 @@
     )
     out = pl.pallas_call(
         kernel,
-        out_shape=jax.ShapeDtypeStruct((planes, outputs, lanes), BF16),
-        in_specs=[pl.BlockSpec(memory_space=pltpu.VMEM)] * 7,
+        out_shape=jax.ShapeDtypeStruct((b * planes * m, outputs * columns), BF16),
+        in_specs=[pl.BlockSpec(memory_space=pltpu.VMEM)] * 8,
         out_specs=pl.BlockSpec(memory_space=pltpu.VMEM),
         scratch_shapes=[
             pltpu.VMEM((6, 128, lanes), BF16),
@@ -239,11 +255,11 @@
             pltpu.VMEM((2, 2, 3, 48, lanes), F32),
             pltpu.VMEM((planes + 4, 240, lanes), BF16),
             pltpu.VMEM((planes + 2, 96, lanes), BF16),
+            pltpu.VMEM((2, b * planes * m * outputs, 128), F32),
         ],
         compiler_params=pltpu.CompilerParams(vmem_limit_bytes=48 * 1024 * 1024),
         name="volume_and_convolutions",
-    )(gathered, far, near, w1, w2, bias_first[:, None], bias_second[:, None])
-    out = out.reshape(planes, outputs, m, b, columns).transpose(3, 0, 2, 1, 4)
+    )(gathered, rests, far, near, w1, w2, bias_first[None, :], bias_second[None, :])
     return out.reshape(b, planes, m, outputs * columns)
 
 

time: 37 us -> 35.6 us (0.962)
  the two profiles are of different devices: /device:TPU:281 before, /device:TPU:1 now
where the time goes in v4:
time: 35.6 us; the launch traced here: 35.3 us
  blocking collectives  12.6 us (35%)
  local copies, waits for them, and re-layouts  7.47 us (21%)
  waiting for transfers between devices  6.22 us (17%)
  Pallas kernels  5.89 us (17%)
  starting transfers between devices  2.58 us (7%)
    all_gather x1, blocking collectives, body(): weights = lax.all_gather(small, 'rows', axis_index_groups=pairs)  8.35 us
    ppermute x2, waiting for transfers between devices, send(): return lax.ppermute(x, ('depth', 'rows'), routes)  6.22 us
    pallas_call x1, Pallas kernels, body(): pl.pallas_call(kernel, out_shape=jax.ShapeDtypeStruct((b * planes * m, ou...  5.89 us
    unnamed x23, local copies, waits for them, and re-layouts  3.94 us
    ppermute x2, starting transfers between devices, send(): return lax.ppermute(x, ('depth', 'rows'), routes)  2.58 us
    all_gather x1, blocking collectives, body(): gathered = lax.all_gather(own, 'rows', axis_index_groups=pairs)  2.16 us
    all_gather x1, blocking collectives, body(): near = lax.all_gather(near, 'rows', axis_index_groups=pairs)  2.04 us
    reshape x1, local copies, waits for them, and re-layouts, body(): return out.reshape(b, planes, m, outputs * columns)  0.79 us
  transfers between devices with their start and end apart: 2, of which 2 were waited for; matrix products, arithmetic and copies ran while one was open for 7% of the time, Pallas kernels for 0%

profile of v4, /device:TPU:1, one launch (start us, length us, event | category | flops | bytes accessed | tf_op | source)
XLA Modules:
  0.0 35.3 jit_solution(8212903671642112133)
XLA Ops:
  0.0 0.0 copy-start.7
  0.0 0.0 copy-start.5
  0.0 0.7 %copy-done.7 = s32[2,4,6,1]{2,3,1,0:T(1,128)S(1)} copy-done((s32[2,4,6,1]{2,3,1,0:T(1,128)S(1)}, s32[2,4,6,1]{2,3,1,0:T(1,128)}, u32[]{:S(2)}) %copy-start.7) | copy-done | bytes 216
  0.7 0.1 copy.19
  0.8 0.1 broadcast_in_dim.16
  0.9 0.1 copy.20
  1.0 0.1 broadcast_bitcast_fusion
  1.1 0.1 reshape.42
  1.2 0.0 copy-done.5
  1.3 0.0 copy-start.2
  1.3 0.1 reshape.41
  1.4 8.4 %all-gather = bf16[64,640]{1,0:T(8,128)(2,1)S(1)} all-gather(bf16[32,640]{1,0:T(8,128)(2,1)S(1)} %fusion.3), channel_id=2, replica_groups={{0,1},{2,3},{4,5},{6,7},{8,9},{10,11},{12,13},{14,15},{16,17},{18,19},{..., dimensions={0}, use_global_device_ids=true | all-gather | bytes 122880 | tf_op jit(solution)/shard_map/all_gather | solution.py:209
  9.8 1.3 %collective-permute-start = (bf16[2,16,640]{2,1,0:T(8,128)(2,1)S(1)}, bf16[2,16,640]{2,1,0:T(8,128)(2,1)S(1)}, u32[]{:S(2)}, u32[]{:S(2)}) collective-permute-start(bf16[2,16,640]{2,1,0:T(8,128)(2,1)S(1)} %fusion.2), channel_id=1, source_target_pairs={{0,16},{2,18},{4,20},{6,22},{8,24},{10,26},{12,28},{14,30},{16,32}... | collective-permute-start | bytes 122888 | tf_op jit(solution)/shard_map/ppermute | solution.py:201
  11.1 0.0 copy-done.2
  11.1 0.1 slice.66
  11.2 0.0 copy-start.6
  11.3 0.1 copy.28
  11.4 0.6 %copy-done.6 = bf16[2,2,5120]{2,1,0:T(2,128)(2,1)S(1)} copy-done((bf16[2,2,5120]{2,1,0:T(2,128)(2,1)S(1)}, bf16[2,2,5120]{2,1,0:T(2,128)(2,1)}, u32[]{:S(2)}) %copy-start.6) | copy-done | bytes 40984
  12.0 0.1 reshape_broadcast_in_dim.3
  12.1 0.1 copy.17
  12.2 0.1 reshape.40
  12.3 0.2 copy.27
  12.5 0.0 copy-start.4
  12.5 0.9 %copy-done.4 = bf16[2,4,2,5120]{3,2,1,0:T(2,128)(2,1)S(1)} copy-done((bf16[2,4,2,5120]{3,2,1,0:T(2,128)(2,1)S(1)}, bf16[2,4,2,5120]{3,2,1,0:T(2,128)(2,1)}, u32[]{:S(2)}) %copy-start.4) | copy-done | bytes 163864
  13.4 0.3 reshape.38
  13.7 0.3 copy.16
  14.0 0.2 reshape.39
  14.2 0.1 pad.12.clone
  14.3 0.3 collective-permute-done
  14.6 2.2 %all-gather.1 = bf16[384,640]{1,0:T(8,128)(2,1)S(1)} all-gather(bf16[192,640]{1,0:T(8,128)(2,1)S(1)} %pad_maximum_fusion.1), channel_id=3, replica_groups={{0,1},{2,3},{4,5},{6,7},{8,9},{10,11},{12,13},{14,15},{16,17},{18,19},{..., dimensions={0}, use_global_device_ids=true | all-gather | bytes 737280 | tf_op jit(solution)/shard_map/all_gather | solution.py:222
  16.9 1.3 %collective-permute-start.1 = (bf16[336,640]{1,0:T(8,128)(2,1)S(1)}, bf16[336,640]{1,0:T(8,128)(2,1)S(1)}, u32[]{:S(2)}, u32[]{:S(2)}) collective-permute-start(bf16[336,640]{1,0:T(8,128)(2,1)S(1)} %pad_maximum_fusion), channel_id=1, source_target_pairs={{0,2},{2,4},{3,1},{4,6},{5,3},{6,8},{7,5},{8,10},{9,7},{10,12},{11... | collective-permute-start | bytes 1290248 | tf_op jit(solution)/shard_map/ppermute | solution.py:201
  18.3 0.1 maximum_bitcast_fusion
  18.4 0.2 copy.24
  18.6 0.0 copy-start.3
  18.6 0.2 reshape.46.w1_ref
  18.8 0.7 %copy-done.3 = bf16[3,3,3,32,32]{4,3,2,1,0:T(8,128)(2,1)S(1)} copy-done((bf16[3,3,3,32,32]{4,3,2,1,0:T(8,128)(2,1)S(1)}, bf16[3,3,3,32,32]{4,3,2,1,0:T(8,128)(2,1)}, u32[]{:S(2)}) %copy-start.3) | copy-done | bytes 55320
  19.5 0.2 copy.25
  19.7 0.2 reshape.47.w2_ref
  19.9 5.9 %collective-permute-done.1.far_ref = bf16[336,640]{1,0:T(8,128)(2,1)S(1)} collective-permute-done((bf16[336,640]{1,0:T(8,128)(2,1)S(1)}, bf16[336,640]{1,0:T(8,128)(2,1)S(1)}, u32[]{:S(2)}, u32[]{:S(2)}) %collective-permute-start.1) | collective-permute-done | bytes 430112 | tf_op jit(solution)/shard_map/ppermute | solution.py:201
  25.9 2.0 %all-gather.2 = bf16[256,640]{1,0:T(8,128)(2,1)S(1)} all-gather(bf16[128,640]{1,0:T(8,128)(2,1)S(1)} %constant_dynamic-slice_fusion), channel_id=4, replica_groups={{0,1},{2,3},{4,5},{6,7},{8,9},{10,11},{12,13},{14,15},{16,17},{18,19},{..., dimensions={0}, use_global_device_ids=true | all-gather | bytes 491520 | tf_op jit(solution)/shard_map/all_gather | solution.py:230
  27.9 0.0 copy-start
  27.9 0.0 copy-start.1
  27.9 0.7 %copy-done = f32[32]{0:T(128)S(1)} copy-done((f32[32]{0:T(128)S(1)}, f32[32]{0:T(128)}, u32[]{:S(2)}) %copy-start) | copy-done | bytes 152
  28.6 0.0 copy-done.1
  28.6 5.9 %volume_and_convolutions.1 = bf16[24,5120]{1,0:T(8,128)(2,1)S(1)} custom-call(bf16[2,192,640]{2,1,0:T(8,128)(2,1)S(1)} %bitcast.39, bf16[2,80,640]{2,1,0:T(8,128)(2,1)S(1)} %maximum_dynamic-update-slice_fusion.rest_ref, bf16[336,640]{1,0:T(8,128)(2,1)S(1)} %collective-permute-done.1.far_ref, bf16[2,128,640]{2,1,0:T(8,128)(2,1)S(1)} %bitcast.40, ...), custom_call_target="tpu_custom_call" | custom-call | tf_op jit(solution)/shard_map/volume_and_convolutions/pallas_call | solution.py:242
  34.5 0.8 %reshape.48 = bf16[2,6,2,5120]{3,2,1,0:T(2,128)(2,1)} reshape(bf16[24,5120]{1,0:T(8,128)(2,1)S(1)} %volume_and_convolutions.1) | data formatting | bytes 491520 | tf_op jit(solution)/shard_map/reshape | solution.py:263
  (24 shorter events, 0.3 us)
Async XLA Ops:
  0.0 0.7 %copy-start.7 = (s32[2,4,6,1]{2,3,1,0:T(1,128)S(1)}, s32[2,4,6,1]{2,3,1,0:T(1,128)}, u32[]{:S(2)}) copy-start(s32[2,4,6,1]{2,3,1,0:T(1,128)} %param.10) | copy-start | bytes 580
  0.0 1.2 %copy-start.5 = (bf16[2,4,6,2,160]{4,3,2,1,0:T(2,128)(2,1)S(1)}, bf16[2,4,6,2,160]{4,3,2,1,0:T(2,128)(2,1)}, u32[]{:S(2)}) copy-start(bf16[2,4,6,2,160]{4,3,2,1,0:T(2,128)(2,1)} %param.11) | copy-start | bytes 92164
  1.3 9.8 %copy-start.2 = (bf16[3,3,3,32,40]{4,3,2,1,0:T(8,128)(2,1)S(1)}, bf16[3,3,3,32,40]{4,3,2,1,0:T(8,128)(2,1)}, u32[]{:S(2)}) copy-start(bf16[3,3,3,32,40]{4,3,2,1,0:T(8,128)(2,1)} %param.12) | copy-start | bytes 207364
  9.8 4.7 %collective-permute-start = (bf16[2,16,640]{2,1,0:T(8,128)(2,1)S(1)}, bf16[2,16,640]{2,1,0:T(8,128)(2,1)S(1)}, u32[]{:S(2)}, u32[]{:S(2)}) collective-permute-start(bf16[2,16,640]{2,1,0:T(8,128)(2,1)S(1)} %fusion.2), channel_id=1, source_target_pairs={{0,16},{2,18},{4,20},{6,22},{8,24},{10,26},{12,28},{14,30},{16,32}... | collective-permute-start | bytes 122888 | tf_op jit(solution)/shard_map/ppermute | solution.py:201
  11.2 0.8 %copy-start.6 = (bf16[2,2,5120]{2,1,0:T(2,128)(2,1)S(1)}, bf16[2,2,5120]{2,1,0:T(2,128)(2,1)}, u32[]{:S(2)}) copy-start(bf16[2,2,5120]{2,1,0:T(2,128)(2,1)} %param.8) | copy-start | bytes 122884
  12.5 0.9 %copy-start.4 = (bf16[2,4,2,5120]{3,2,1,0:T(2,128)(2,1)S(1)}, bf16[2,4,2,5120]{3,2,1,0:T(2,128)(2,1)}, u32[]{:S(2)}) copy-start(bf16[2,4,2,5120]{3,2,1,0:T(2,128)(2,1)} %param.9) | copy-start | bytes 491524
  16.9 8.9 %collective-permute-start.1 = (bf16[336,640]{1,0:T(8,128)(2,1)S(1)}, bf16[336,640]{1,0:T(8,128)(2,1)S(1)}, u32[]{:S(2)}, u32[]{:S(2)}) collective-permute-start(bf16[336,640]{1,0:T(8,128)(2,1)S(1)} %pad_maximum_fusion), channel_id=1, source_target_pairs={{0,2},{2,4},{3,1},{4,6},{5,3},{6,8},{7,5},{8,10},{9,7},{10,12},{11... | collective-permute-start | bytes 1290248 | tf_op jit(solution)/shard_map/ppermute | solution.py:201
  18.6 0.9 %copy-start.3 = (bf16[3,3,3,32,32]{4,3,2,1,0:T(8,128)(2,1)S(1)}, bf16[3,3,3,32,32]{4,3,2,1,0:T(8,128)(2,1)}, u32[]{:S(2)}) copy-start(bf16[3,3,3,32,32]{4,3,2,1,0:T(8,128)(2,1)} %param.14) | copy-start | bytes 165892
  27.9 0.7 %copy-start = (f32[32]{0:T(128)S(1)}, f32[32]{0:T(128)}, u32[]{:S(2)}) copy-start(f32[32]{0:T(128)} %param.13) | copy-start | bytes 388
  27.9 0.7 %copy-start.1 = (f32[32]{0:T(128)S(1)}, f32[32]{0:T(128)}, u32[]{:S(2)}) copy-start(f32[32]{0:T(128)} %param.15) | copy-start | bytes 388

commit v5 on v4

--- a/solution.py
+++ b/solution.py
@@ -23,7 +23,7 @@
 
 
 def compute_kernel(
-    own_ref, rest_ref, far_ref, near_ref, w1_ref, w2_ref, b1_ref, b2_ref, out_ref,
+    own_ref, rest_ref, far_ref, near_ref, w1_ref, w2_ref, out_ref,
     src_ref, rf_ref, tm_ref, tp_ref, e0_ref, dm_ref, dp_ref, vf_ref, v_ref, h_ref, o_ref,
     *, planes, columns, depth_count, row_count,
 ):
@@ -59,8 +59,8 @@
             b1 = jnp.where(half, turned, o)
             tiles = lanes // 128
             below = jnp.where(scene, jnp.concatenate([b1] * tiles, axis=1), jnp.concatenate([b0] * tiles, axis=1)) < -0.5
-            tm_ref[r, 8 * i : 8 * i + 8, :] = jnp.where(below, w, 0.0)
-            tp_ref[r, 8 * i : 8 * i + 8, :] = jnp.where(below, 0.0, 1.0 - w)
+            tm_ref[r, 8 * i : 8 * i + 8, :] = jnp.where(below, w, 1.0 - w)
+            tp_ref[r, 8 * i : 8 * i + 8, :] = jnp.where(below, 1.0, 0.0)
 
     for k in range(3):
         base = rf_ref[core + k]
@@ -94,8 +94,10 @@
                     squares = jnp.zeros((32, 128), F32)
                     for v in range(views):
                         n = views * t + v
-                        e = e0_ref[k, v, :, cols] + tm[n : n + 1] * dm_ref[k, v, :, cols]
-                        e = e + tp[n : n + 1] * dp_ref[k, v, :, cols]
+                        upper = jnp.broadcast_to(tp[n : n + 1], (8, 128)) > 0.5
+                        upper = jnp.concatenate([upper] * 4, axis=0)
+                        step = jnp.where(upper, dm_ref[k, v, :, cols], dp_ref[k, v, :, cols])
+                        e = e0_ref[k, v, :, cols] + tm[n : n + 1] * step
                         total = total + e
                         squares = squares + e * e
                     spread = squares * (0.2 * keep) - total * total * (0.04 * keep)
@@ -111,7 +113,8 @@
                 between = mixed(vf_ref[pair % 2, t, k], vf_ref[pair % 2, t, k + 1])
                 v_ref[p, 96 * k + 48 : 96 * k + 96, :] = between.astype(BF16)
 
-    vf_ref[:, :, :, 40:48, :] = jnp.zeros((2, 2, 3, 8, lanes), F32)
+    vf_ref[:, :, :, 40:48, :] = jnp.ones((2, 2, 3, 8, lanes), F32)
+    ones = jnp.ones((16, lanes), BF16)
 
     def shifted_sum(parts, width):
         column = jnp.concatenate([col] * (width // lanes), axis=1)
@@ -126,10 +129,6 @@
         ],
         axis=1,
     )
-
-    diagonal = lax.broadcasted_iota(jnp.int32, (32, 32), 0) == lax.broadcasted_iota(jnp.int32, (32, 32), 1)
-    bias_first = jnp.sum(jnp.where(diagonal, b1_ref[...], 0.0), axis=1, keepdims=True)
-    bias_second = jnp.sum(jnp.where(diagonal, b2_ref[...], 0.0), axis=1, keepdims=True)
 
     def hidden_plane(p):
         upper = jnp.concatenate([v_ref[p + a, 0:144, :] for a in range(3)], axis=0)
@@ -141,7 +140,7 @@
             keep = keep * jnp.where(first, 0.0, 1.0).astype(F32)
         if p == planes + 1:
             keep = keep * jnp.where(last, 0.0, 1.0).astype(F32)
-        hidden = jnp.maximum(shifted_sum(parts, 2 * lanes) + bias_first, 0.0) * keep
+        hidden = jnp.maximum(shifted_sum(parts, 2 * lanes), 0.0) * keep
         above = hidden[:, :lanes]
         below = hidden[:, lanes:]
         h_ref[p, 0:32, :] = above.astype(BF16)
@@ -149,9 +148,9 @@
         h_ref[p, 64:96, :] = below.astype(BF16)
 
     def out_plane(p):
-        taps = jnp.concatenate([h_ref[p + a] for a in range(3)], axis=0)
+        taps = jnp.concatenate([h_ref[p + a] for a in range(3)] + [ones], axis=0)
         parts = jnp.dot(w2_ref[...], taps, preferred_element_type=F32)
-        result = shifted_sum(parts, lanes) + bias_second
+        result = shifted_sum(parts, lanes)
         for m in range(2):
             for b in range(2):
                 at = 32 * ((b * planes + p) * 2 + m)
@@ -174,7 +173,8 @@
             for j in range(4):
                 rows = pl.ds(256 * g + 4 * a + j, 8, stride=32)
                 pieces += [o_ref[0, rows, :], o_ref[1, rows, :][:, : columns - 128]]
-            out_ref[8 * g : 8 * g + 8, 4 * columns * a : 4 * columns * (a + 1)] = jnp.concatenate(pieces, axis=1).astype(BF16)
+            values = jnp.concatenate(pieces, axis=1).reshape(4, 2, 4 * columns).astype(BF16)
+            out_ref[4 * g : 4 * g + 4, :, 4 * columns * a : 4 * columns * (a + 1)] = values
 
 
 def body(ref_feat, src_feat, block_index, blend, conv_first, bias_first, conv_second, bias_second):
@@ -229,20 +229,27 @@
     near = lax.dynamic_slice_in_dim(far, 128 * (1 - core), 128, 0)
     near = lax.all_gather(near, "rows", axis_index_groups=pairs)
 
+    def split(bias):
+        high = lax.reduce_precision(bias, 8, 7)
+        middle = lax.reduce_precision(bias - high, 8, 7)
+        return jnp.stack([high, middle, bias - high - middle], axis=1).astype(BF16)
+
     corr = conv_first[..., :groups] * jnp.asarray(0.0625, BF16)
     spread = conv_first[..., groups:].reshape(3, 3, 3, outputs, groups, per_group)
     spread = spread.swapaxes(4, 5).reshape(3, 3, 3, outputs, feat)
-    padded = jnp.concatenate([spread, corr, jnp.zeros_like(corr)], axis=-1)
+    centre = jnp.pad(split(bias_first)[None, None, None], ((1, 1), (1, 1), (1, 1), (0, 0), (0, groups - 3)))
+    padded = jnp.concatenate([spread, corr, centre], axis=-1)
     w1 = padded.transpose(2, 3, 0, 1, 4).reshape(3 * outputs, -1)
     w2 = conv_second.transpose(2, 3, 0, 1, 4).reshape(3 * outputs, -1)
+    w2 = jnp.concatenate([w2, jnp.pad(split(bias_second), ((outputs, outputs), (0, 13)))], axis=1)
 
     kernel = functools.partial(
         compute_kernel, planes=planes, columns=columns, depth_count=depth_count, row_count=row_count
     )
     out = pl.pallas_call(
         kernel,
-        out_shape=jax.ShapeDtypeStruct((b * planes * m, outputs * columns), BF16),
-        in_specs=[pl.BlockSpec(memory_space=pltpu.VMEM)] * 8,
+        out_shape=jax.ShapeDtypeStruct((b * planes, m, outputs * columns), BF16),
+        in_specs=[pl.BlockSpec(memory_space=pltpu.VMEM)] * 6,
         out_specs=pl.BlockSpec(memory_space=pltpu.VMEM),
         scratch_shapes=[
             pltpu.VMEM((6, 128, lanes), BF16),
@@ -259,7 +266,7 @@
         ],
         compiler_params=pltpu.CompilerParams(vmem_limit_bytes=48 * 1024 * 1024),
         name="volume_and_convolutions",
-    )(gathered, rests, far, near, w1, w2, bias_first[None, :], bias_second[None, :])
+    )(gathered, rests, far, near, w1, w2)
     return out.reshape(b, planes, m, outputs * columns)
 
 

time: 35.6 us -> 34.9 us (0.980)
  local copies, waits for them, and re-layouts: 7.47 us -> 6.05 us
  Pallas kernels: 5.89 us -> 6.64 us
    reshape x1 -> x0, local copies, waits for them, and re-layouts: 0.79 us -> none  [body(): return out.reshape(b, planes, m, outputs * columns)]
    pallas_call x1, Pallas kernels: 5.89 us -> 6.64 us  [body(): pl.pallas_call(kernel, out_shape=jax.ShapeDtypeStruct((b * planes, m, out...]
    unnamed x23, local copies, waits for them, and re-layouts: 3.94 us -> 3.28 us
where the time goes in v5:
time: 34.9 us; the launch traced here: 34.6 us
  blocking collectives  12.6 us (36%)
  Pallas kernels  6.64 us (19%)
  waiting for transfers between devices  6.1 us (17%)
  local copies, waits for them, and re-layouts  6.05 us (17%)
  starting transfers between devices  2.58 us (7%)
    all_gather x1, blocking collectives, body(): weights = lax.all_gather(small, 'rows', axis_index_groups=pairs)  8.35 us
    pallas_call x1, Pallas kernels, body(): pl.pallas_call(kernel, out_shape=jax.ShapeDtypeStruct((b * planes, m, out...  6.64 us
    ppermute x2, waiting for transfers between devices, send(): return lax.ppermute(x, ('depth', 'rows'), routes)  6.1 us
    unnamed x23, local copies, waits for them, and re-layouts  3.28 us
    ppermute x2, starting transfers between devices, send(): return lax.ppermute(x, ('depth', 'rows'), routes)  2.58 us
    all_gather x1, blocking collectives, body(): gathered = lax.all_gather(own, 'rows', axis_index_groups=pairs)  2.16 us
    all_gather x1, blocking collectives, body(): near = lax.all_gather(near, 'rows', axis_index_groups=pairs)  2.04 us
  transfers between devices with their start and end apart: 2, of which 2 were waited for; matrix products, arithmetic and copies ran while one was open for 7% of the time, Pallas kernels for 0%

profile of v5, /device:TPU:1, one launch (start us, length us, event | category | flops | bytes accessed | tf_op | source)
XLA Modules:
  0.0 34.6 jit_solution(11929572704935301398)
XLA Ops:
  0.0 0.0 copy-start.5
  0.0 0.0 copy-start.3
  0.0 0.7 %copy-done.5 = s32[2,4,6,1]{2,3,1,0:T(1,128)S(1)} copy-done((s32[2,4,6,1]{2,3,1,0:T(1,128)S(1)}, s32[2,4,6,1]{2,3,1,0:T(1,128)}, u32[]{:S(2)}) %copy-start.5) | copy-done | bytes 216
  0.7 0.1 copy.36
  0.8 0.1 broadcast_in_dim.8
  0.9 0.1 copy.37
  1.0 0.1 broadcast_bitcast_fusion
  1.1 0.1 reshape.90
  1.2 0.0 copy-done.3
  1.3 0.0 copy-start
  1.3 0.1 reshape.89
  1.4 8.4 %all-gather = bf16[64,640]{1,0:T(8,128)(2,1)S(1)} all-gather(bf16[32,640]{1,0:T(8,128)(2,1)S(1)} %fusion.16), channel_id=2, replica_groups={{0,1},{2,3},{4,5},{6,7},{8,9},{10,11},{12,13},{14,15},{16,17},{18,19},{..., dimensions={0}, use_global_device_ids=true | all-gather | bytes 122880 | tf_op jit(solution)/shard_map/all_gather | solution.py:209
  9.8 0.0 copy-start.6
  9.8 0.0 copy-start.7
  9.8 1.3 %collective-permute-start = (bf16[2,16,640]{2,1,0:T(8,128)(2,1)S(1)}, bf16[2,16,640]{2,1,0:T(8,128)(2,1)S(1)}, u32[]{:S(2)}, u32[]{:S(2)}) collective-permute-start(bf16[2,16,640]{2,1,0:T(8,128)(2,1)S(1)} %fusion.15), channel_id=1, source_target_pairs={{0,16},{2,18},{4,20},{6,22},{8,24},{10,26},{12,28},{14,30},{16,32}... | collective-permute-start | bytes 122888 | tf_op jit(solution)/shard_map/ppermute | solution.py:201
  11.1 0.0 copy-done.6
  11.1 0.0 copy-done.7
  11.2 0.1 copy.43
  11.3 0.0 copy-done
  11.3 0.1 slice.66
  11.4 0.0 copy-start.4
  11.4 0.1 copy.46
  11.6 0.6 %copy-done.4 = bf16[2,2,5120]{2,1,0:T(2,128)(2,1)S(1)} copy-done((bf16[2,2,5120]{2,1,0:T(2,128)(2,1)S(1)}, bf16[2,2,5120]{2,1,0:T(2,128)(2,1)}, u32[]{:S(2)}) %copy-start.4) | copy-done | bytes 40984
  12.2 0.1 reshape_broadcast_in_dim.3
  12.3 0.1 copy.34
  12.4 0.1 reshape.88
  12.5 0.2 copy.45
  12.7 0.0 copy-start.2
  12.7 0.9 %copy-done.2 = bf16[2,4,2,5120]{3,2,1,0:T(2,128)(2,1)S(1)} copy-done((bf16[2,4,2,5120]{3,2,1,0:T(2,128)(2,1)S(1)}, bf16[2,4,2,5120]{3,2,1,0:T(2,128)(2,1)}, u32[]{:S(2)}) %copy-start.2) | copy-done | bytes 163864
  13.6 0.3 reshape.86
  13.9 0.3 copy.33
  14.1 0.2 reshape.87
  14.4 0.2 collective-permute-done
  14.6 2.2 %all-gather.1 = bf16[384,640]{1,0:T(8,128)(2,1)S(1)} all-gather(bf16[192,640]{1,0:T(8,128)(2,1)S(1)} %pad_maximum_fusion.1), channel_id=3, replica_groups={{0,1},{2,3},{4,5},{6,7},{8,9},{10,11},{12,13},{14,15},{16,17},{18,19},{..., dimensions={0}, use_global_device_ids=true | all-gather | bytes 737280 | tf_op jit(solution)/shard_map/all_gather | solution.py:222
  17.0 1.3 %collective-permute-start.1 = (bf16[336,640]{1,0:T(8,128)(2,1)S(1)}, bf16[336,640]{1,0:T(8,128)(2,1)S(1)}, u32[]{:S(2)}, u32[]{:S(2)}) collective-permute-start(bf16[336,640]{1,0:T(8,128)(2,1)S(1)} %pad_maximum_fusion), channel_id=1, source_target_pairs={{0,2},{2,4},{3,1},{4,6},{5,3},{6,8},{7,5},{8,10},{9,7},{10,12},{11... | collective-permute-start | bytes 1290248 | tf_op jit(solution)/shard_map/ppermute | solution.py:201
  18.3 0.1 maximum_bitcast_fusion
  18.4 0.2 copy.41
  18.6 0.0 copy-start.1
  18.6 0.2 reshape.94.w1_ref
  18.8 0.7 %copy-done.1 = bf16[3,3,3,32,32]{4,3,2,1,0:T(8,128)(2,1)S(1)} copy-done((bf16[3,3,3,32,32]{4,3,2,1,0:T(8,128)(2,1)S(1)}, bf16[3,3,3,32,32]{4,3,2,1,0:T(8,128)(2,1)}, u32[]{:S(2)}) %copy-start.1) | copy-done | bytes 55320
  19.5 0.2 copy.42
  19.7 0.2 reshape.95
  19.9 0.1 fusion.9.w2_ref
  20.0 5.9 %collective-permute-done.1.far_ref = bf16[336,640]{1,0:T(8,128)(2,1)S(1)} collective-permute-done((bf16[336,640]{1,0:T(8,128)(2,1)S(1)}, bf16[336,640]{1,0:T(8,128)(2,1)S(1)}, u32[]{:S(2)}, u32[]{:S(2)}) %collective-permute-start.1) | collective-permute-done | bytes 430112 | tf_op jit(solution)/shard_map/ppermute | solution.py:201
  25.9 2.0 %all-gather.2 = bf16[256,640]{1,0:T(8,128)(2,1)S(1)} all-gather(bf16[128,640]{1,0:T(8,128)(2,1)S(1)} %constant_dynamic-slice_fusion), channel_id=4, replica_groups={{0,1},{2,3},{4,5},{6,7},{8,9},{10,11},{12,13},{14,15},{16,17},{18,19},{..., dimensions={0}, use_global_device_ids=true | all-gather | bytes 491520 | tf_op jit(solution)/shard_map/all_gather | solution.py:230
  27.9 6.6 %volume_and_convolutions.1 = bf16[12,2,5120]{2,1,0:T(2,128)(2,1)} custom-call(bf16[2,192,640]{2,1,0:T(8,128)(2,1)S(1)} %bitcast.50, bf16[2,80,640]{2,1,0:T(8,128)(2,1)S(1)} %maximum_dynamic-update-slice_fusion.rest_ref, bf16[336,640]{1,0:T(8,128)(2,1)S(1)} %collective-permute-done.1.far_ref, bf16[2,128,640]{2,1,0:T(8,128)(2,1)S(1)} %bitcast.51, ...), custom_call_target="tpu_custom_call" | custom-call | tf_op jit(solution)/shard_map/volume_and_convolutions/pallas_call | solution.py:249
  (26 shorter events, 0.4 us)
Async XLA Ops:
  0.0 0.7 %copy-start.5 = (s32[2,4,6,1]{2,3,1,0:T(1,128)S(1)}, s32[2,4,6,1]{2,3,1,0:T(1,128)}, u32[]{:S(2)}) copy-start(s32[2,4,6,1]{2,3,1,0:T(1,128)} %param.10) | copy-start | bytes 580
  0.0 1.2 %copy-start.3 = (bf16[2,4,6,2,160]{4,3,2,1,0:T(2,128)(2,1)S(1)}, bf16[2,4,6,2,160]{4,3,2,1,0:T(2,128)(2,1)}, u32[]{:S(2)}) copy-start(bf16[2,4,6,2,160]{4,3,2,1,0:T(2,128)(2,1)} %param.11) | copy-start | bytes 92164
  1.3 10.0 %copy-start = (bf16[3,3,3,32,40]{4,3,2,1,0:T(8,128)(2,1)S(1)}, bf16[3,3,3,32,40]{4,3,2,1,0:T(8,128)(2,1)}, u32[]{:S(2)}) copy-start(bf16[3,3,3,32,40]{4,3,2,1,0:T(8,128)(2,1)} %param.12) | copy-start | bytes 207364
  9.8 1.3 %copy-start.6 = (f32[32]{0:T(128)S(1)}, f32[32]{0:T(128)}, u32[]{:S(2)}) copy-start(f32[32]{0:T(128)} %param.13) | copy-start | bytes 388
  9.8 1.3 %copy-start.7 = (f32[32]{0:T(128)S(1)}, f32[32]{0:T(128)}, u32[]{:S(2)}) copy-start(f32[32]{0:T(128)} %param.15) | copy-start | bytes 388
  9.8 4.7 %collective-permute-start = (bf16[2,16,640]{2,1,0:T(8,128)(2,1)S(1)}, bf16[2,16,640]{2,1,0:T(8,128)(2,1)S(1)}, u32[]{:S(2)}, u32[]{:S(2)}) collective-permute-start(bf16[2,16,640]{2,1,0:T(8,128)(2,1)S(1)} %fusion.15), channel_id=1, source_target_pairs={{0,16},{2,18},{4,20},{6,22},{8,24},{10,26},{12,28},{14,30},{16,32}... | collective-permute-start | bytes 122888 | tf_op jit(solution)/shard_map/ppermute | solution.py:201
  11.4 0.8 %copy-start.4 = (bf16[2,2,5120]{2,1,0:T(2,128)(2,1)S(1)}, bf16[2,2,5120]{2,1,0:T(2,128)(2,1)}, u32[]{:S(2)}) copy-start(bf16[2,2,5120]{2,1,0:T(2,128)(2,1)} %param.8) | copy-start | bytes 122884
  12.7 0.9 %copy-start.2 = (bf16[2,4,2,5120]{3,2,1,0:T(2,128)(2,1)S(1)}, bf16[2,4,2,5120]{3,2,1,0:T(2,128)(2,1)}, u32[]{:S(2)}) copy-start(bf16[2,4,2,5120]{3,2,1,0:T(2,128)(2,1)} %param.9) | copy-start | bytes 491524
  17.0 8.9 %collective-permute-start.1 = (bf16[336,640]{1,0:T(8,128)(2,1)S(1)}, bf16[336,640]{1,0:T(8,128)(2,1)S(1)}, u32[]{:S(2)}, u32[]{:S(2)}) collective-permute-start(bf16[336,640]{1,0:T(8,128)(2,1)S(1)} %pad_maximum_fusion), channel_id=1, source_target_pairs={{0,2},{2,4},{3,1},{4,6},{5,3},{6,8},{7,5},{8,10},{9,7},{10,12},{11... | collective-permute-start | bytes 1290248 | tf_op jit(solution)/shard_map/ppermute | solution.py:201
  18.6 0.9 %copy-start.1 = (bf16[3,3,3,32,32]{4,3,2,1,0:T(8,128)(2,1)S(1)}, bf16[3,3,3,32,32]{4,3,2,1,0:T(8,128)(2,1)}, u32[]{:S(2)}) copy-start(bf16[3,3,3,32,32]{4,3,2,1,0:T(8,128)(2,1)} %param.14) | copy-start | bytes 165892

commit v6 on v5

--- a/solution.py
+++ b/solution.py
@@ -90,16 +90,14 @@
                 tp = tp_ref[core + k, row : row + 8, cols]
                 base = rf_ref[core + k, :, cols]
                 for t in range(2):
-                    total = jnp.zeros((32, 128), F32)
-                    squares = jnp.zeros((32, 128), F32)
                     for v in range(views):
                         n = views * t + v
                         upper = jnp.broadcast_to(tp[n : n + 1], (8, 128)) > 0.5
                         upper = jnp.concatenate([upper] * 4, axis=0)
                         step = jnp.where(upper, dm_ref[k, v, :, cols], dp_ref[k, v, :, cols])
                         e = e0_ref[k, v, :, cols] + tm[n : n + 1] * step
-                        total = total + e
-                        squares = squares + e * e
+                        total = e if v == 0 else total + e
+                        squares = e * e if v == 0 else squares + e * e
                     spread = squares * (0.2 * keep) - total * total * (0.04 * keep)
                     product = base * (total + 4.0 * base)
                     corr = (product[0:8] + product[8:16] + product[16:24] + product[24:32]) * keep

time: 34.9 us -> 34.9 us (level)
  no operation moved by 1% of the time
where the time goes in v6:
time: 34.9 us; the launch traced here: 34.6 us
  blocking collectives  12.6 us (36%)
  Pallas kernels  6.64 us (19%)
  waiting for transfers between devices  6.1 us (17%)
  local copies, waits for them, and re-layouts  6.05 us (17%)
  starting transfers between devices  2.58 us (7%)
    all_gather x1, blocking collectives, body(): weights = lax.all_gather(small, 'rows', axis_index_groups=pairs)  8.35 us
    pallas_call x1, Pallas kernels, body(): pl.pallas_call(kernel, out_shape=jax.ShapeDtypeStruct((b * planes, m, out...  6.64 us
    ppermute x2, waiting for transfers between devices, send(): return lax.ppermute(x, ('depth', 'rows'), routes)  6.1 us
    unnamed x23, local copies, waits for them, and re-layouts  3.28 us
    ppermute x2, starting transfers between devices, send(): return lax.ppermute(x, ('depth', 'rows'), routes)  2.58 us
    all_gather x1, blocking collectives, body(): gathered = lax.all_gather(own, 'rows', axis_index_groups=pairs)  2.16 us
    all_gather x1, blocking collectives, body(): near = lax.all_gather(near, 'rows', axis_index_groups=pairs)  2.04 us
  transfers between devices with their start and end apart: 2, of which 2 were waited for; matrix products, arithmetic and copies ran while one was open for 7% of the time, Pallas kernels for 0%

profile of v6, /device:TPU:1, one launch (start us, length us, event | category | flops | bytes accessed | tf_op | source)
XLA Modules:
  0.0 34.6 jit_solution(11929572704935301398)
XLA Ops:
  0.0 0.0 copy-start.5
  0.0 0.0 copy-start.3
  0.0 0.7 %copy-done.5 = s32[2,4,6,1]{2,3,1,0:T(1,128)S(1)} copy-done((s32[2,4,6,1]{2,3,1,0:T(1,128)S(1)}, s32[2,4,6,1]{2,3,1,0:T(1,128)}, u32[]{:S(2)}) %copy-start.5) | copy-done | bytes 216
  0.7 0.1 copy.36
  0.8 0.1 broadcast_in_dim.8
  0.9 0.1 copy.37
  1.0 0.1 broadcast_bitcast_fusion
  1.1 0.1 reshape.90
  1.2 0.0 copy-done.3
  1.3 0.0 copy-start
  1.3 0.1 reshape.89
  1.4 8.4 %all-gather = bf16[64,640]{1,0:T(8,128)(2,1)S(1)} all-gather(bf16[32,640]{1,0:T(8,128)(2,1)S(1)} %fusion.16), channel_id=2, replica_groups={{0,1},{2,3},{4,5},{6,7},{8,9},{10,11},{12,13},{14,15},{16,17},{18,19},{..., dimensions={0}, use_global_device_ids=true | all-gather | bytes 122880 | tf_op jit(solution)/shard_map/all_gather | solution.py:207
  9.8 0.0 copy-start.6
  9.8 0.0 copy-start.7
  9.8 1.3 %collective-permute-start = (bf16[2,16,640]{2,1,0:T(8,128)(2,1)S(1)}, bf16[2,16,640]{2,1,0:T(8,128)(2,1)S(1)}, u32[]{:S(2)}, u32[]{:S(2)}) collective-permute-start(bf16[2,16,640]{2,1,0:T(8,128)(2,1)S(1)} %fusion.15), channel_id=1, source_target_pairs={{0,16},{2,18},{4,20},{6,22},{8,24},{10,26},{12,28},{14,30},{16,32}... | collective-permute-start | bytes 122888 | tf_op jit(solution)/shard_map/ppermute | solution.py:199
  11.1 0.0 copy-done.6
  11.1 0.0 copy-done.7
  11.2 0.1 copy.43
  11.3 0.0 copy-done
  11.3 0.1 slice.66
  11.4 0.0 copy-start.4
  11.4 0.1 copy.46
  11.6 0.6 %copy-done.4 = bf16[2,2,5120]{2,1,0:T(2,128)(2,1)S(1)} copy-done((bf16[2,2,5120]{2,1,0:T(2,128)(2,1)S(1)}, bf16[2,2,5120]{2,1,0:T(2,128)(2,1)}, u32[]{:S(2)}) %copy-start.4) | copy-done | bytes 40984
  12.2 0.1 reshape_broadcast_in_dim.3
  12.3 0.1 copy.34
  12.4 0.1 reshape.88
  12.5 0.2 copy.45
  12.7 0.0 copy-start.2
  12.7 0.9 %copy-done.2 = bf16[2,4,2,5120]{3,2,1,0:T(2,128)(2,1)S(1)} copy-done((bf16[2,4,2,5120]{3,2,1,0:T(2,128)(2,1)S(1)}, bf16[2,4,2,5120]{3,2,1,0:T(2,128)(2,1)}, u32[]{:S(2)}) %copy-start.2) | copy-done | bytes 163864
  13.6 0.3 reshape.86
  13.9 0.3 copy.33
  14.1 0.2 reshape.87
  14.4 0.2 collective-permute-done
  14.6 2.2 %all-gather.1 = bf16[384,640]{1,0:T(8,128)(2,1)S(1)} all-gather(bf16[192,640]{1,0:T(8,128)(2,1)S(1)} %pad_maximum_fusion.1), channel_id=3, replica_groups={{0,1},{2,3},{4,5},{6,7},{8,9},{10,11},{12,13},{14,15},{16,17},{18,19},{..., dimensions={0}, use_global_device_ids=true | all-gather | bytes 737280 | tf_op jit(solution)/shard_map/all_gather | solution.py:220
  17.0 1.3 %collective-permute-start.1 = (bf16[336,640]{1,0:T(8,128)(2,1)S(1)}, bf16[336,640]{1,0:T(8,128)(2,1)S(1)}, u32[]{:S(2)}, u32[]{:S(2)}) collective-permute-start(bf16[336,640]{1,0:T(8,128)(2,1)S(1)} %pad_maximum_fusion), channel_id=1, source_target_pairs={{0,2},{2,4},{3,1},{4,6},{5,3},{6,8},{7,5},{8,10},{9,7},{10,12},{11... | collective-permute-start | bytes 1290248 | tf_op jit(solution)/shard_map/ppermute | solution.py:199
  18.3 0.1 maximum_bitcast_fusion
  18.4 0.2 copy.41
  18.6 0.0 copy-start.1
  18.6 0.2 reshape.94.w1_ref
  18.8 0.7 %copy-done.1 = bf16[3,3,3,32,32]{4,3,2,1,0:T(8,128)(2,1)S(1)} copy-done((bf16[3,3,3,32,32]{4,3,2,1,0:T(8,128)(2,1)S(1)}, bf16[3,3,3,32,32]{4,3,2,1,0:T(8,128)(2,1)}, u32[]{:S(2)}) %copy-start.1) | copy-done | bytes 55320
  19.5 0.2 copy.42
  19.7 0.2 reshape.95
  19.9 0.1 fusion.9.w2_ref
  20.0 5.9 %collective-permute-done.1.far_ref = bf16[336,640]{1,0:T(8,128)(2,1)S(1)} collective-permute-done((bf16[336,640]{1,0:T(8,128)(2,1)S(1)}, bf16[336,640]{1,0:T(8,128)(2,1)S(1)}, u32[]{:S(2)}, u32[]{:S(2)}) %collective-permute-start.1) | collective-permute-done | bytes 430112 | tf_op jit(solution)/shard_map/ppermute | solution.py:199
  25.9 2.0 %all-gather.2 = bf16[256,640]{1,0:T(8,128)(2,1)S(1)} all-gather(bf16[128,640]{1,0:T(8,128)(2,1)S(1)} %constant_dynamic-slice_fusion), channel_id=4, replica_groups={{0,1},{2,3},{4,5},{6,7},{8,9},{10,11},{12,13},{14,15},{16,17},{18,19},{..., dimensions={0}, use_global_device_ids=true | all-gather | bytes 491520 | tf_op jit(solution)/shard_map/all_gather | solution.py:228
  27.9 6.6 %volume_and_convolutions.1 = bf16[12,2,5120]{2,1,0:T(2,128)(2,1)} custom-call(bf16[2,192,640]{2,1,0:T(8,128)(2,1)S(1)} %bitcast.50, bf16[2,80,640]{2,1,0:T(8,128)(2,1)S(1)} %maximum_dynamic-update-slice_fusion.rest_ref, bf16[336,640]{1,0:T(8,128)(2,1)S(1)} %collective-permute-done.1.far_ref, bf16[2,128,640]{2,1,0:T(8,128)(2,1)S(1)} %bitcast.51, ...), custom_call_target="tpu_custom_call" | custom-call | tf_op jit(solution)/shard_map/volume_and_convolutions/pallas_call | solution.py:247
  (26 shorter events, 0.4 us)
Async XLA Ops:
  0.0 0.7 %copy-start.5 = (s32[2,4,6,1]{2,3,1,0:T(1,128)S(1)}, s32[2,4,6,1]{2,3,1,0:T(1,128)}, u32[]{:S(2)}) copy-start(s32[2,4,6,1]{2,3,1,0:T(1,128)} %param.10) | copy-start | bytes 580
  0.0 1.2 %copy-start.3 = (bf16[2,4,6,2,160]{4,3,2,1,0:T(2,128)(2,1)S(1)}, bf16[2,4,6,2,160]{4,3,2,1,0:T(2,128)(2,1)}, u32[]{:S(2)}) copy-start(bf16[2,4,6,2,160]{4,3,2,1,0:T(2,128)(2,1)} %param.11) | copy-start | bytes 92164
  1.3 10.0 %copy-start = (bf16[3,3,3,32,40]{4,3,2,1,0:T(8,128)(2,1)S(1)}, bf16[3,3,3,32,40]{4,3,2,1,0:T(8,128)(2,1)}, u32[]{:S(2)}) copy-start(bf16[3,3,3,32,40]{4,3,2,1,0:T(8,128)(2,1)} %param.12) | copy-start | bytes 207364
  9.8 1.3 %copy-start.6 = (f32[32]{0:T(128)S(1)}, f32[32]{0:T(128)}, u32[]{:S(2)}) copy-start(f32[32]{0:T(128)} %param.13) | copy-start | bytes 388
  9.8 1.3 %copy-start.7 = (f32[32]{0:T(128)S(1)}, f32[32]{0:T(128)}, u32[]{:S(2)}) copy-start(f32[32]{0:T(128)} %param.15) | copy-start | bytes 388
  9.8 4.7 %collective-permute-start = (bf16[2,16,640]{2,1,0:T(8,128)(2,1)S(1)}, bf16[2,16,640]{2,1,0:T(8,128)(2,1)S(1)}, u32[]{:S(2)}, u32[]{:S(2)}) collective-permute-start(bf16[2,16,640]{2,1,0:T(8,128)(2,1)S(1)} %fusion.15), channel_id=1, source_target_pairs={{0,16},{2,18},{4,20},{6,22},{8,24},{10,26},{12,28},{14,30},{16,32}... | collective-permute-start | bytes 122888 | tf_op jit(solution)/shard_map/ppermute | solution.py:199
  11.4 0.8 %copy-start.4 = (bf16[2,2,5120]{2,1,0:T(2,128)(2,1)S(1)}, bf16[2,2,5120]{2,1,0:T(2,128)(2,1)}, u32[]{:S(2)}) copy-start(bf16[2,2,5120]{2,1,0:T(2,128)(2,1)} %param.8) | copy-start | bytes 122884
  12.7 0.9 %copy-start.2 = (bf16[2,4,2,5120]{3,2,1,0:T(2,128)(2,1)S(1)}, bf16[2,4,2,5120]{3,2,1,0:T(2,128)(2,1)}, u32[]{:S(2)}) copy-start(bf16[2,4,2,5120]{3,2,1,0:T(2,128)(2,1)} %param.9) | copy-start | bytes 491524
  17.0 8.9 %collective-permute-start.1 = (bf16[336,640]{1,0:T(8,128)(2,1)S(1)}, bf16[336,640]{1,0:T(8,128)(2,1)S(1)}, u32[]{:S(2)}, u32[]{:S(2)}) collective-permute-start(bf16[336,640]{1,0:T(8,128)(2,1)S(1)} %pad_maximum_fusion), channel_id=1, source_target_pairs={{0,2},{2,4},{3,1},{4,6},{5,3},{6,8},{7,5},{8,10},{9,7},{10,12},{11... | collective-permute-start | bytes 1290248 | tf_op jit(solution)/shard_map/ppermute | solution.py:199
  18.6 0.9 %copy-start.1 = (bf16[3,3,3,32,32]{4,3,2,1,0:T(8,128)(2,1)S(1)}, bf16[3,3,3,32,32]{4,3,2,1,0:T(8,128)(2,1)}, u32[]{:S(2)}) copy-start(bf16[3,3,3,32,32]{4,3,2,1,0:T(8,128)(2,1)} %param.14) | copy-start | bytes 165892
